TPU v7x, 128 devices: a whole 4x4x4 slice. The times are simulated.
128 devices in a mesh: band: 8 (over y, core), tile: 16 (over z, x).
Axes of the slice: x: 4, y: 4, z: 4, core: 2. Of those that a mesh axis runs over, the one named last changes fastest.
Arguments:
- patches: bfloat16 [1048576, 128], P(('band', 'tile')), may hold values from -6 to 6
- pair_patch: int32 [16384], P(('band', 'tile')), may hold values from 0 to 63
- pair_atm: int32 [16384], P(('band', 'tile')), may hold values from 0 to 16383, as said below
- numerators: int32 [16384, 128, 32], P(('band', 'tile')), may hold values from 0 to 16777215
- counts: int32 [128], P(('band', 'tile')), may hold values from 32 to 128, as said below
Outputs:
- atmosphere: float32 [524288, 128], P(('band', 'tile'))
Inputs may be any that keep to these rules, and one draw needn't show every extreme that they name: Block pair_atm[g] is owned by device pair_atm[g] // 128 (band-major device order). Every live pair of device (b, t) targets an owner in band b (any tile) or one of (b - 1, t), (b + 1, t). Among one device's live pairs at most 32 target one owner and at most 16 distinct blocks of one owner; both are reached on some device in every draw. Slots that are not live hold arbitrary blocks in range. `counts`: the value 128 occurs on some device in every draw.
All inputs are finite; a program needn't handle non-finite values.
Results may differ from a plain program's by a relative error of at most 0.0026.
Values sent between devices are 32-bit elements; how exact they have to be, the bound alone decides.
A program may use at most 64 MiB of HBM per device.

v0:
```python
import jax
import jax.numpy as jnp
from jax import lax
from jax.sharding import PartitionSpec as P

CELLS_DEV = 4096


SCALE = 2.0 ** (-27)


def shifted(value, axis, steps):
    count = lax.axis_size(axis)
    first, last = (max(0, -steps), min(count, count - steps))
    return lax.ppermute(value, axis, [(source, source + steps) for source in range(first, last)])


def slot_ranks(owners, blocks_local, live_pairs):
    position = jnp.arange(owners.shape[0])
    earlier = position[None, :] < position[:, None]
    both_live = live_pairs[None, :] & live_pairs[:, None]
    same_owner = (owners[:, None] == owners[None, :]) & both_live
    same_block = same_owner & (blocks_local[:, None] == blocks_local[None, :])
    leading = jnp.logical_not(jnp.any(same_block & earlier, axis=1))
    leader_rank = jnp.sum((same_owner & earlier & leading[None, :]).astype(jnp.int32), axis=1)
    first_match = same_block & leading[None, :]
    return jnp.sum(jnp.where(first_match, leader_rank[None, :], 0), axis=1)


def pack(flattened, rows_index, selected, blocks_local, rows_total):
    onehot = (rows_index[None, :] == jnp.arange(rows_total)[:, None]) & selected[None, :]
    payload = jnp.dot(onehot.astype(jnp.float32), flattened, precision=lax.Precision.HIGHEST)
    labels = jnp.max(jnp.where(onehot, blocks_local[None, :], -1), axis=1)
    return (payload, labels)


def unpack(payload, labels, blocks_owned):
    onehot = (labels[None, :] == jnp.arange(blocks_owned)[:, None]).astype(jnp.float32)
    return jnp.dot(onehot, payload, precision=lax.Precision.HIGHEST)


def along_band(parcel, offset_by):
    return shifted((parcel[0], parcel[1]), "band", offset_by)


def per_device(patches, pair_patch, pair_atm, numerators, counts):
    pairs_here, patch_rows, cell_rows = numerators.shape
    flux_width = patches.shape[1]
    blocks_owned = CELLS_DEV // cell_rows
    capacity = pairs_here // 4
    grouped = patches.reshape(-1, patch_rows, flux_width)
    live_pairs = jnp.arange(pairs_here) < counts[0]
    weight = (numerators.astype(jnp.float32) * SCALE).astype(jnp.bfloat16)
    chosen = grouped[pair_patch]
    partial_value = jnp.einsum("jpa,jpf->jaf", weight, chosen, preferred_element_type=jnp.float32)
    flattened = partial_value.reshape(pairs_here, cell_rows * flux_width)
    owners = pair_atm // blocks_owned
    blocks_local = pair_atm % blocks_owned
    slot_rank = slot_ranks(owners, blocks_local, live_pairs)
    bucket_size = capacity // 2
    tile_count = lax.axis_size("tile")
    band_now = lax.axis_index("band")
    tile_now = lax.axis_index("tile")
    owner_band = owners // tile_count
    owner_tile = owners % tile_count
    in_band = live_pairs & (owner_band == band_now)
    rows_index = jnp.where(in_band, owner_tile * bucket_size + slot_rank, -1)
    payload, labels = pack(flattened, rows_index, in_band, blocks_local, tile_count * bucket_size)

    def bucket(target):
        addressed = live_pairs & (owners == target)
        target_rows = jnp.where(addressed, slot_rank, -1)
        return pack(flattened, target_rows, addressed, blocks_local, bucket_size)

    upper_index = (band_now + 1) * tile_count + tile_now
    lower_index = (band_now - 1) * tile_count + tile_now
    from_below = along_band(bucket(upper_index), 1)
    from_above = along_band(bucket(lower_index), -1)
    band_payload = jnp.concatenate([from_below[0], from_above[0]], axis=0)
    band_labels = jnp.concatenate([from_below[1], from_above[1]], axis=0)
    payload, labels = (
        lax.all_to_all(
            payload.reshape(tile_count, bucket_size, -1),
            "tile",
            split_axis=0,
            concat_axis=0,
            tiled=True,
        ),
        lax.all_to_all(
            labels.reshape(tile_count, bucket_size), "tile", split_axis=0, concat_axis=0, tiled=True
        ),
    )
    payload = jnp.concatenate([payload.reshape(tile_count * bucket_size, -1), band_payload], axis=0)
    labels = jnp.concatenate([labels.reshape(-1), band_labels], axis=0)
    summed = unpack(payload, labels, blocks_owned)
    return summed.reshape(blocks_owned * cell_rows, flux_width)


def solution(mesh):
    placed = (
        P(("band", "tile"), None),
        P(("band", "tile")),
        P(("band", "tile")),
        P(("band", "tile"), None, None),
        P(("band", "tile")),
    )
    return jax.shard_map(
        per_device, mesh=mesh, in_specs=placed, out_specs=P(("band", "tile"), None), check_vma=False
    )
```

profile of v0, /device:TPU:0, one launch (start us, length us, event | category | flops | bytes accessed | tf_op | source)
XLA Modules:
  0.0 105.7 jit_solution(7318644868519810167)
XLA Ops:
  0.0 0.0 copy-start
  0.8 0.7 and_select_fusion
  1.5 0.2 fusion.23
  1.7 0.2 convert_reduce_fusion
  1.9 0.2 select_reduce_fusion.1
  2.1 0.1 select_reduce_fusion
  2.2 0.7 all_to_all.9
  2.9 8.0 %all-to-all-start = ((s32[16,1,16]{2,1,0:T(1,128)}), s32[16,1,16]{2,1,0:T(1,128)S(1)}, u32[]{:S(2)}, u32[]{:S(2)}) async-start(s32[16,1,16]{2,1,0:T(1,128)} %all_to_all.9), calls=%async_computation | async-start | bytes 16384 | tf_op jit(solution)/shard_map/all_to_all | solution.py:89
  10.9 0.7 compare_select_fusion
  11.6 0.0 copy-done
  11.6 3.0 %gather_fusion = bf16[128,128,128]{2,1,0:T(8,128)(2,1)} fusion(bf16[64,128,128]{2,1,0:T(8,128)(2,1)S(1)} %bitcast.13, s32[1024]{0:T(1024)S(1)} %pad_clamp_fusion), kind=kCustom, calls=%fused_computation | custom fusion | bytes 8389120 | tf_op jit(solution)/shard_map/gather | solution.py:54
  14.6 5.3 %fusion.12 = f32[128,32,128]{2,1,0:T(8,128)} fusion(bf16[128,128,128]{2,1,0:T(8,128)(2,1)} %gather_fusion, s32[128,128,32]{1,2,0:T(8,128)} %param.8), kind=kOutput, calls=%fused_computation.14 | convolution fusion | flops 135790592 | bytes 8388608 | tf_op jit(solution)/shard_map/jpa,jpf->jaf/dot_general | solution.py:55
  20.0 2.7 %reshape.80 = f32[128,4096,1]{1,0,2:T(8,128)} reshape(f32[128,32,128]{2,1,0:T(8,128)} %fusion.12) | data formatting | bytes 4194304 | tf_op jit(solution)/shard_map/reshape | solution.py:56
  22.7 5.4 %fusion.15 = f32[16,16,4096]{2,1,0:T(8,128)} fusion(f32[128,4096,1]{1,0,2:T(8,128)} %reshape.80, s32[16,16]{1,0:T(8,128)S(1)} %multiply_add_fusion, s32[128]{0:T(128)S(1)} %get-tuple-element.7, pred[128]{0:T(512)(128)(4,1)S(1)} %get-tuple-element.8), kind=kOutput, calls=%fused_computation.20 | convolution fusion | flops 1610678272 | bytes 6293120 | tf_op jit(solution)/shard_map/dot_general | solution.py:32
  28.1 0.0 all-to-all-done
  28.1 7.3 %all-to-all-start.1 = ((f32[16,16,4096]{2,1,0:T(8,128)}), f32[16,16,4096]{2,1,0:T(8,128)}, u32[]{:S(2)}, u32[]{:S(2)}) async-start(f32[16,16,4096]{2,1,0:T(8,128)} %fusion.15), calls=%async_computation.1 | async-start | bytes 8388608 | tf_op jit(solution)/shard_map/all_to_all | solution.py:82
  35.4 0.0 copy-start.1
  35.4 3.6 %fusion.8 = f32[16,4096]{1,0:T(8,128)S(1)} fusion(f32[16,8,32,128]{3,2,1,0:T(8,128)} %bitcast.14, s32[128]{0:T(128)S(1)} %get-tuple-element.13, pred[128]{0:T(512)(128)(4,1)S(1)} %get-tuple-element.14), kind=kOutput, calls=%fused_computation.9 | convolution fusion | flops 100667392 | bytes 2359936 | tf_op jit(solution)/shard_map/dot_general | solution.py:32
  39.0 1.3 %collective-permute-start.3 = (f32[16,4096]{1,0:T(8,128)S(1)}, f32[16,4096]{1,0:T(8,128)S(1)}, u32[]{:S(2)}, u32[]{:S(2)}) collective-permute-start(f32[16,4096]{1,0:T(8,128)S(1)} %fusion.8), channel_id=1, source_target_pairs={{16,0},{32,16},{48,32},{64,48},{80,64},{96,80},{112,96},{17,1},{33... | collective-permute-start | bytes 786440 | tf_op jit(solution)/shard_map/ppermute | solution.py:15
  40.3 0.0 copy-done.1
  40.3 2.0 %fusion.6 = f32[16,4096]{1,0:T(8,128)S(1)} fusion(f32[16,8,32,128]{3,2,1,0:T(8,128)S(1)} %bitcast.15, s32[128]{0:T(128)S(1)} %get-tuple-element.15, pred[128]{0:T(512)(128)(4,1)S(1)} %get-tuple-element.16), kind=kOutput, calls=%fused_computation.7 | convolution fusion | flops 100667392 | bytes 2359936 | tf_op jit(solution)/shard_map/dot_general | solution.py:32
  42.3 3.0 %collective-permute-start.2 = (f32[16,4096]{1,0:T(8,128)S(1)}, f32[16,4096]{1,0:T(8,128)S(1)}, u32[]{:S(2)}, u32[]{:S(2)}) collective-permute-start(f32[16,4096]{1,0:T(8,128)S(1)} %fusion.6), channel_id=1, source_target_pairs={{0,16},{16,32},{32,48},{48,64},{64,80},{80,96},{96,112},{1,17},{17... | collective-permute-start | bytes 786440 | tf_op jit(solution)/shard_map/ppermute | solution.py:15
  45.3 0.1 select_reduce_fusion.3
  45.4 3.1 %collective-permute-start = (s32[16]{0:T(128)S(1)}, s32[16]{0:T(128)S(1)}, u32[]{:S(2)}, u32[]{:S(2)}) collective-permute-start(s32[16]{0:T(128)S(1)} %get-tuple-element.5), channel_id=1, source_target_pairs={{0,16},{16,32},{32,48},{48,64},{64,80},{80,96},{96,112},{1,17},{17... | collective-permute-start | bytes 200 | tf_op jit(solution)/shard_map/ppermute | solution.py:15
  48.5 1.3 %collective-permute-start.1 = (s32[16]{0:T(128)S(1)}, s32[16]{0:T(128)S(1)}, u32[]{:S(2)}, u32[]{:S(2)}) collective-permute-start(s32[16]{0:T(128)S(1)} %get-tuple-element.6), channel_id=1, source_target_pairs={{16,0},{32,16},{48,32},{64,48},{80,64},{96,80},{112,96},{17,1},{33... | collective-permute-start | bytes 200 | tf_op jit(solution)/shard_map/ppermute | solution.py:15
  49.8 0.5 broadcast.108
  50.3 0.7 reduce.3
  51.0 0.1 reshape.66
  51.1 0.0 collective-permute-done
  51.1 0.5 collective-permute-done.1
  51.6 0.1 pad_add_fusion
  51.7 0.0 collective-permute-done.3
  51.7 0.0 collective-permute-done.2
  51.7 45.4 %all-to-all-done.1 = f32[16,16,4096]{2,1,0:T(8,128)} async-done(((f32[16,16,4096]{2,1,0:T(8,128)}), f32[16,16,4096]{2,1,0:T(8,128)}, u32[]{:S(2)}, u32[]{:S(2)}) %all-to-all-start.1) | async-done | bytes 4194336 | tf_op jit(solution)/shard_map/all_to_all | solution.py:82
  97.1 5.9 %fusion = f32[128,4096]{1,0:T(8,128)} fusion(f32[16,4096]{1,0:T(8,128)S(1)} %collective-permute-done.3, f32[16,4096]{1,0:T(8,128)S(1)} %collective-permute-done.2, f32[256,4096]{1,0:T(8,128)} %bitcast.2, s32[288]{0:T(512)S(1)} %pad_add_fusion), kind=kOutput, calls=%fused_computation.1 | convolution fusion | flops 1814335488 | bytes 6816896 | tf_op jit(solution)/shard_map/dot_general | solution.py:39
  103.0 2.7 %reshape.70 = f32[4096,128]{1,0:T(8,128)} reshape(f32[128,4096]{1,0:T(8,128)} %fusion) | data formatting | bytes 4194304 | tf_op jit(solution)/shard_map/reshape | solution.py:96
  (5 shorter events, 0.0 us)
Async XLA Ops:
  0.0 11.6 %copy-start = (bf16[8192,128]{1,0:T(8,128)(2,1)S(1)}, bf16[8192,128]{1,0:T(8,128)(2,1)}, u32[]{:S(2)}) copy-start(bf16[8192,128]{1,0:T(8,128)(2,1)} %param.5) | copy-start | bytes 6291460
  2.9 25.2 %all-to-all-start = ((s32[16,1,16]{2,1,0:T(1,128)}), s32[16,1,16]{2,1,0:T(1,128)S(1)}, u32[]{:S(2)}, u32[]{:S(2)}) async-start(s32[16,1,16]{2,1,0:T(1,128)} %all_to_all.9), calls=%async_computation | async-start | bytes 16384 | tf_op jit(solution)/shard_map/all_to_all | solution.py:89
  28.1 69.0 %all-to-all-start.1 = ((f32[16,16,4096]{2,1,0:T(8,128)}), f32[16,16,4096]{2,1,0:T(8,128)}, u32[]{:S(2)}, u32[]{:S(2)}) async-start(f32[16,16,4096]{2,1,0:T(8,128)} %fusion.15), calls=%async_computation.1 | async-start | bytes 8388608 | tf_op jit(solution)/shard_map/all_to_all | solution.py:82
  35.4 4.9 %copy-start.1 = (f32[128,32,128]{2,1,0:T(8,128)S(1)}, f32[128,32,128]{2,1,0:T(8,128)}, u32[]{:S(2)}) copy-start(f32[128,32,128]{2,1,0:T(8,128)} %fusion.12) | copy-start | bytes 6291460
  39.0 12.7 %collective-permute-start.3 = (f32[16,4096]{1,0:T(8,128)S(1)}, f32[16,4096]{1,0:T(8,128)S(1)}, u32[]{:S(2)}, u32[]{:S(2)}) collective-permute-start(f32[16,4096]{1,0:T(8,128)S(1)} %fusion.8), channel_id=1, source_target_pairs={{16,0},{32,16},{48,32},{64,48},{80,64},{96,80},{112,96},{17,1},{33... | collective-permute-start | bytes 786440 | tf_op jit(solution)/shard_map/ppermute | solution.py:15
  42.3 9.4 %collective-permute-start.2 = (f32[16,4096]{1,0:T(8,128)S(1)}, f32[16,4096]{1,0:T(8,128)S(1)}, u32[]{:S(2)}, u32[]{:S(2)}) collective-permute-start(f32[16,4096]{1,0:T(8,128)S(1)} %fusion.6), channel_id=1, source_target_pairs={{0,16},{16,32},{32,48},{48,64},{64,80},{80,96},{96,112},{1,17},{17... | collective-permute-start | bytes 786440 | tf_op jit(solution)/shard_map/ppermute | solution.py:15
  45.4 5.7 %collective-permute-start = (s32[16]{0:T(128)S(1)}, s32[16]{0:T(128)S(1)}, u32[]{:S(2)}, u32[]{:S(2)}) collective-permute-start(s32[16]{0:T(128)S(1)} %get-tuple-element.5), channel_id=1, source_target_pairs={{0,16},{16,32},{32,48},{48,64},{64,80},{80,96},{96,112},{1,17},{17... | collective-permute-start | bytes 200 | tf_op jit(solution)/shard_map/ppermute | solution.py:15
  48.5 3.1 %collective-permute-start.1 = (s32[16]{0:T(128)S(1)}, s32[16]{0:T(128)S(1)}, u32[]{:S(2)}, u32[]{:S(2)}) collective-permute-start(s32[16]{0:T(128)S(1)} %get-tuple-element.6), channel_id=1, source_target_pairs={{16,0},{32,16},{48,32},{64,48},{80,64},{96,80},{112,96},{17,1},{33... | collective-permute-start | bytes 200 | tf_op jit(solution)/shard_map/ppermute | solution.py:15
where the time goes:
time: 106 us
  waiting for transfers between devices  45.9 us (43%)
  starting transfers between devices  24 us (23%)
  matrix products  22.2 us (21%)
  local copies, waits for them, and re-layouts  9.75 us (9%)
  other arithmetic  2.95 us (3%)
    all_to_all x1, waiting for transfers between devices, per_device(): lax.all_to_all(payload.reshape(tile_count, bucket_size, -1), 'tile', spli...  45.4 us
    dot_general x3, matrix products, pack(): jnp.dot(onehot.astype(jnp.float32), flattened, precision=lax.Precision.HI...  10.9 us
    ppermute x4, starting transfers between devices, shifted(): lax.ppermute(value, axis, [(source, source + steps) for source in range(f...  8.72 us
    all_to_all x1, starting transfers between devices, per_device(): lax.all_to_all(labels.reshape(tile_count, bucket_size), 'tile', split_axi...  7.99 us
    all_to_all x1, starting transfers between devices, per_device(): lax.all_to_all(payload.reshape(tile_count, bucket_size, -1), 'tile', spli...  7.26 us
    dot_general x1, matrix products, unpack(): return jnp.dot(onehot, payload, precision=lax.Precision.HIGHEST)  5.89 us
    dot_general x1, matrix products, per_device(): jnp.einsum('jpa,jpf->jaf', weight, chosen, preferred_element_type=jnp.flo...  5.35 us
    gather x1, local copies, waits for them, and re-layouts, per_device(): chosen = grouped[pair_patch]  3.01 us
  transfers between devices with their start and end apart: 6, of which 2 were waited for; matrix products, arithmetic and copies ran while one was open for 23% of the time, Pallas kernels for 0%

commit v1 on v0

--- a/solution.py
+++ b/solution.py
@@ -1,12 +1,474 @@
+import functools
+
 import jax
 import jax.numpy as jnp
 from jax import lax
+from jax.experimental import pallas as pl
+from jax.experimental.pallas import tpu as pltpu
 from jax.sharding import PartitionSpec as P
 
 CELLS_DEV = 4096
-
-
 SCALE = 2.0 ** (-27)
+
+TILES = 16
+BANDS = 8
+PAIRS = 128
+CELLS = 32
+LANES = 128
+BLOCKS = 128
+NEAR = 16
+FAR0 = 3 * NEAR
+NC = 32
+DC = 72
+PIECE = CELLS // TILES
+MESH = pl.DeviceIdType.MESH
+F32, BF16, I32 = jnp.float32, jnp.bfloat16, jnp.int32
+
+
+def iota(shape, axis):
+    return lax.broadcasted_iota(I32, shape, axis)
+
+
+def split(value):
+    high = value.astype(BF16)
+    return high, (value - high.astype(F32)).astype(BF16)
+
+
+def exchange_kernel(
+    counts_ref, patch_ref, atm_ref, num_hbm, patches_hbm,
+    far_ref, near_ref, place_ref, flag_ref,
+    num_v, pat_v, part, send_far, send_up, send_down, relay, stacked, parcel,
+    note, notes, alarm, alarms,
+    in_sem, note_send, note_recv, r_send, r_recv, q_send, q_recv,
+    near_send, near_recv, alarm_send, alarm_recv,
+):
+    band, tile = lax.axis_index("band"), lax.axis_index("tile")
+    chunks = in_sem.shape[0] - 1
+    rows = PAIRS // chunks
+
+    def tile_at(k):
+        return lax.rem(tile + k, TILES)
+
+    def band_at(k):
+        return lax.rem(band + k, BANDS)
+
+    pat_copy = pltpu.make_async_copy(patches_hbm, pat_v, in_sem.at[chunks])
+    pat_copy.start()
+    num_copies = [
+        pltpu.make_async_copy(
+            num_hbm.at[pl.ds(i * rows, rows)], num_v.at[pl.ds(i * rows, rows)], in_sem.at[i]
+        )
+        for i in range(chunks)
+    ]
+    for copy in num_copies:
+        copy.start()
+
+    barrier = pltpu.get_barrier_semaphore()
+
+    @pl.loop(1, TILES)
+    def _(k):
+        pl.semaphore_signal(barrier, inc=1, device_id={"tile": tile_at(k)}, device_id_type=MESH)
+
+    @pl.loop(1, BANDS)
+    def _(k):
+        pl.semaphore_signal(barrier, inc=1, device_id={"band": band_at(k)}, device_id_type=MESH)
+
+    lane, sub = iota((PAIRS, LANES), 1), iota((PAIRS, LANES), 0)
+    lane1 = iota((1, LANES), 1)
+
+    def column(row):
+        return jnp.sum(jnp.where(lane == sub, row, 0.0), axis=1, keepdims=True)
+
+    atm = atm_ref[...]
+    live = lane1 < counts_ref[0]
+    owner = atm >> 7
+    me = band * TILES + tile
+    base = jnp.where(
+        owner == me,
+        0,
+        jnp.where(owner == me + TILES, NEAR, jnp.where(owner == me - TILES, 2 * NEAR, FAR0)),
+    ).astype(F32)
+    key = jnp.where(live, atm, -1).astype(F32)
+    key_c, base_c = column(key), column(base)
+    same = (key_c == key) & (key >= 0.0)
+    earlier = jnp.sum(jnp.where(same & (sub < lane), 1.0, 0.0), axis=0, keepdims=True)
+    first = jnp.where(live & (earlier == 0.0), 1.0, 0.0)
+    first_c = column(first)
+    ahead = (first_c > 0.0) & (base_c == base) & (key_c < key)
+    rank = jnp.sum(jnp.where(ahead, 1.0, 0.0), axis=0, keepdims=True)
+    slot = jnp.where(live, base + rank, -1.0)
+    slot_c = column(slot).astype(I32)
+    leads = first_c > 0.0
+    key_i = key_c.astype(I32)
+    far_lane = slot_c - FAR0 + NC * lax.rem(tile, 4)
+    in_far = leads & (slot_c >= FAR0) & (slot_c < FAR0 + NC)
+    far_label = (key_i - band * (TILES * BLOCKS) + 1).astype(F32)
+    far_row = jnp.sum(jnp.where(in_far & (far_lane == lane), far_label, 0.0), axis=0, keepdims=True)
+    in_near = leads & (slot_c < FAR0) & (slot_c == lane)
+    near_label = ((key_i & (BLOCKS - 1)) + 1).astype(F32)
+    near_row = jnp.sum(jnp.where(in_near, near_label, 0.0), axis=0, keepdims=True)
+    n_far = jnp.sum(jnp.where(base == FAR0, first, 0.0), axis=1, keepdims=True)
+    note[0:1, :] = far_row
+    note[1:2, :] = jnp.where(lane1 == LANES - 1, n_far, near_row)
+
+    @pl.when(band == 0)
+    def _():
+        notes[TILES] = jnp.zeros((2, LANES), F32)
+        near_ref[1] = jnp.zeros((CELLS, NEAR, LANES), F32)
+
+    @pl.when(band == BANDS - 1)
+    def _():
+        notes[TILES + 1] = jnp.zeros((2, LANES), F32)
+        near_ref[2] = jnp.zeros((CELLS, NEAR, LANES), F32)
+
+    pl.semaphore_wait(barrier, TILES + BANDS - 2)
+
+    def note_to(k):
+        return pltpu.make_async_remote_copy(
+            src_ref=note, dst_ref=notes.at[tile], send_sem=note_send.at[tile_at(k)],
+            recv_sem=note_recv.at[tile], device_id={"tile": tile_at(k)}, device_id_type=MESH,
+        )
+
+    def note_from(k):
+        source = tile_at(TILES - k)
+        return pltpu.make_async_remote_copy(
+            src_ref=note, dst_ref=notes.at[source], send_sem=note_send.at[source],
+            recv_sem=note_recv.at[source], device_id={"tile": source}, device_id_type=MESH,
+        )
+
+    def note_up():
+        return pltpu.make_async_remote_copy(
+            src_ref=note, dst_ref=notes.at[TILES], send_sem=note_send.at[TILES],
+            recv_sem=note_recv.at[TILES], device_id={"band": band_at(1)}, device_id_type=MESH,
+        )
+
+    def note_down():
+        return pltpu.make_async_remote_copy(
+            src_ref=note, dst_ref=notes.at[TILES + 1], send_sem=note_send.at[TILES + 1],
+            recv_sem=note_recv.at[TILES + 1], device_id={"band": band_at(BANDS - 1)},
+            device_id_type=MESH,
+        )
+
+    @pl.loop(1, TILES)
+    def _(k):
+        note_to(k).start()
+
+    @pl.when(band < BANDS - 1)
+    def _():
+        note_up().start()
+
+    @pl.when(band > 0)
+    def _():
+        note_down().start()
+
+    notes[tile] = note[...]
+
+    pat_copy.wait()
+    for i in range(chunks):
+        num_copies[i].wait()
+
+        @pl.loop(0, rows, unroll=8)
+        def _(j):
+            g = i * rows + j
+            weight = num_v[g].astype(F32).astype(BF16)
+            part[pl.ds(g, CELLS, stride=PAIRS), :] = jnp.dot(
+                weight, pat_v[patch_ref[g]], preferred_element_type=F32
+            )
+
+    slot_sub = iota((FAR0 + NC, LANES), 0)
+    pick = jnp.where(slot.astype(I32) == slot_sub, SCALE, 0.0).astype(BF16)
+    pick2 = jnp.concatenate([pick, pick], axis=1)
+
+    def slots_of(m):
+        both = part[pl.ds(m * PIECE * PAIRS, PIECE * PAIRS), :]
+        wide = jnp.concatenate([both[:PAIRS], both[PAIRS:]], axis=1)
+        total = jnp.dot(
+            pick2, jnp.concatenate(split(wide), axis=0), preferred_element_type=F32
+        )
+        for c in range(PIECE):
+            here = total[:, c * LANES : (c + 1) * LANES]
+            near_ref[0, m * PIECE + c] = here[:NEAR]
+            send_up[m * PIECE + c] = here[NEAR : 2 * NEAR]
+            send_down[m * PIECE + c] = here[2 * NEAR : FAR0]
+            send_far[m, c] = here[FAR0:]
+
+    def far_to(k):
+        return pltpu.make_async_remote_copy(
+            src_ref=send_far.at[tile_at(k)], dst_ref=relay.at[tile], send_sem=r_send.at[tile_at(k)],
+            recv_sem=r_recv.at[tile], device_id={"tile": tile_at(k)}, device_id_type=MESH,
+        )
+
+    def far_from(k):
+        source = tile_at(TILES - k)
+        return pltpu.make_async_remote_copy(
+            src_ref=send_far.at[source], dst_ref=relay.at[source], send_sem=r_send.at[source],
+            recv_sem=r_recv.at[source], device_id={"tile": source}, device_id_type=MESH,
+        )
+
+    @pl.loop(1, TILES)
+    def _(k):
+        slots_of(tile_at(k))
+        far_to(k).start()
+
+    slots_of(tile)
+    relay[tile] = send_far[tile]
+
+    def near_up():
+        return pltpu.make_async_remote_copy(
+            src_ref=send_up, dst_ref=near_ref.at[1], send_sem=near_send.at[0],
+            recv_sem=near_recv.at[0], device_id={"band": band_at(1)}, device_id_type=MESH,
+        )
+
+    def near_down():
+        return pltpu.make_async_remote_copy(
+            src_ref=send_down, dst_ref=near_ref.at[2], send_sem=near_send.at[1],
+            recv_sem=near_recv.at[1], device_id={"band": band_at(BANDS - 1)}, device_id_type=MESH,
+        )
+
+    @pl.when(band < BANDS - 1)
+    def _():
+        near_up().start()
+
+    @pl.when(band > 0)
+    def _():
+        near_down().start()
+
+    @pl.loop(1, TILES)
+    def _(k):
+        note_from(k).wait_recv()
+
+    quarters = []
+    for q in range(4):
+        quarters.append(
+            notes[4 * q, 0:1, :] + notes[4 * q + 1, 0:1, :]
+            + notes[4 * q + 2, 0:1, :] + notes[4 * q + 3, 0:1, :]
+        )
+    label = jnp.concatenate(quarters, axis=1).astype(I32)
+    entries = TILES * NC
+    filled = label > 0
+    label = label - 1
+    goes_to, block = label >> 7, label & (BLOCKS - 1)
+    is_block = filled & (iota((BLOCKS, entries), 0) == block)
+    block_hot = jnp.where(is_block, 1.0, 0.0).astype(BF16)
+    owner_hot = jnp.where(
+        filled & (iota((TILES, entries), 0) == goes_to), 1.0, 0.0
+    ).astype(BF16)
+    hits = lax.dot_general(
+        block_hot, owner_hot, (((1,), (1,)), ((), ())), preferred_element_type=F32
+    )
+    taken = jnp.where(hits > 0.0, 1.0, 0.0)
+    below = jnp.where(lane < sub, 1.0, 0.0).astype(BF16)
+    order = jnp.dot(below, taken.astype(BF16), preferred_element_type=F32)
+    spread = jnp.dot(order.astype(BF16), owner_hot, preferred_element_type=F32)
+    depth = jnp.sum(jnp.where(is_block, spread, 0.0), axis=0, keepdims=True).astype(I32)
+    goal = jnp.where(filled & (depth < DC), goes_to * DC + depth, -1)
+
+    most_far = notes[0, 1:2, :]
+    for s in range(1, TILES):
+        most_far = jnp.maximum(most_far, notes[s, 1:2, :])
+    over_far = jnp.max(
+        jnp.where(lane1 == LANES - 1, most_far - NC, 0.0), axis=1, keepdims=True
+    )
+    load = jnp.sum(taken, axis=0, keepdims=True)
+    over_load = jnp.max(load - DC, axis=1, keepdims=True)
+    alarm[...] = jnp.broadcast_to(
+        jnp.where((over_far > 0.0) | (over_load > 0.0), 1.0, 0.0), (1, LANES)
+    )
+
+    def alarm_to(k):
+        return pltpu.make_async_remote_copy(
+            src_ref=alarm, dst_ref=alarms.at[band], send_sem=alarm_send.at[band_at(k)],
+            recv_sem=alarm_recv.at[band], device_id={"band": band_at(k)}, device_id_type=MESH,
+        )
+
+    def alarm_from(k):
+        source = band_at(BANDS - k)
+        return pltpu.make_async_remote_copy(
+            src_ref=alarm, dst_ref=alarms.at[source], send_sem=alarm_send.at[source],
+            recv_sem=alarm_recv.at[source], device_id={"band": source}, device_id_type=MESH,
+        )
+
+    @pl.loop(1, BANDS)
+    def _(k):
+        alarm_to(k).start()
+
+    alarms[band] = alarm[...]
+
+    @pl.when(band > 0)
+    def _():
+        note_up().wait_recv()
+
+    @pl.when(band < BANDS - 1)
+    def _():
+        note_down().wait_recv()
+
+    near_labels = jnp.where(
+        lane1 < NEAR,
+        note[1:2, :],
+        jnp.where(lane1 < 2 * NEAR, notes[TILES, 1:2, :], notes[TILES + 1, 1:2, :]),
+    )
+    mine = iota((BLOCKS, TILES), 1) == tile
+    my_taken = jnp.sum(jnp.where(mine, taken, 0.0), axis=1, keepdims=True)
+    my_order = jnp.sum(jnp.where(mine, order, 0.0), axis=1, keepdims=True).astype(I32)
+    is_near = (lane < FAR0) & (near_labels.astype(I32) == sub + 1)
+    is_far = (lane >= FAR0) & (lane < FAR0 + DC) & (my_taken > 0.0) & (my_order == lane - FAR0)
+    place_ref[...] = jnp.where(is_near | is_far, 1.0, 0.0)
+
+    @pl.loop(1, TILES)
+    def _(k):
+        far_from(k).wait_recv()
+
+    for c in range(PIECE):
+        high, low = split(relay[:, c].reshape(entries, LANES))
+        stacked[:entries, c * LANES : (c + 1) * LANES] = high
+        stacked[entries:, c * LANES : (c + 1) * LANES] = low
+    depth_sub = iota((DC, entries), 0)
+
+    def blocks_of(owner_tile):
+        hot = jnp.where(depth_sub + owner_tile * DC == goal, 1.0, 0.0).astype(BF16)
+        return jnp.dot(
+            jnp.concatenate([hot, hot], axis=1), stacked[...], preferred_element_type=F32
+        )
+
+    def parcel_to(k):
+        return pltpu.make_async_remote_copy(
+            src_ref=parcel.at[tile_at(k)], dst_ref=far_ref.at[tile], send_sem=q_send.at[tile_at(k)],
+            recv_sem=q_recv.at[tile], device_id={"tile": tile_at(k)}, device_id_type=MESH,
+        )
+
+    def parcel_from(k):
+        source = tile_at(TILES - k)
+        return pltpu.make_async_remote_copy(
+            src_ref=parcel.at[source], dst_ref=far_ref.at[source], send_sem=q_send.at[source],
+            recv_sem=q_recv.at[source], device_id={"tile": source}, device_id_type=MESH,
+        )
+
+    @pl.loop(1, TILES)
+    def _(k):
+        total = blocks_of(tile_at(k))
+        for c in range(PIECE):
+            parcel[tile_at(k), c] = total[:, c * LANES : (c + 1) * LANES]
+        parcel_to(k).start()
+
+    own = blocks_of(tile)
+    for c in range(PIECE):
+        far_ref[tile, c] = own[:, c * LANES : (c + 1) * LANES]
+
+    @pl.loop(1, BANDS)
+    def _(k):
+        alarm_from(k).wait_recv()
+
+    flag_ref[0] = jnp.max(alarms[...]).astype(I32)
+
+    @pl.when(band > 0)
+    def _():
+        near_up().wait_recv()
+        note_down().wait_send()
+        near_down().wait_send()
+
+    @pl.when(band < BANDS - 1)
+    def _():
+        near_down().wait_recv()
+        note_up().wait_send()
+        near_up().wait_send()
+
+    @pl.loop(1, BANDS)
+    def _(k):
+        alarm_to(k).wait_send()
+
+    @pl.loop(1, TILES)
+    def _(k):
+        note_to(k).wait_send()
+        far_to(k).wait_send()
+        parcel_from(k).wait_recv()
+
+    @pl.loop(1, TILES)
+    def _(k):
+        parcel_to(k).wait_send()
+
+
+def exchange(patches, pair_patch, pair_atm, numerators, counts):
+    vmem = pl.BlockSpec(memory_space=pltpu.VMEM)
+    smem = pl.BlockSpec(memory_space=pltpu.SMEM)
+    anywhere = pl.BlockSpec(memory_space=pl.ANY)
+    dma = pltpu.SemaphoreType.DMA
+    return pl.pallas_call(
+        exchange_kernel,
+        out_shape=(
+            jax.ShapeDtypeStruct((TILES, PIECE, DC, LANES), F32),
+            jax.ShapeDtypeStruct((3, CELLS, NEAR, LANES), F32),
+            jax.ShapeDtypeStruct((BLOCKS, LANES), F32),
+            jax.ShapeDtypeStruct((1,), I32),
+        ),
+        in_specs=[smem, smem, vmem, anywhere, anywhere],
+        out_specs=(vmem, vmem, vmem, smem),
+        scratch_shapes=[
+            pltpu.VMEM((PAIRS, CELLS, LANES), I32),
+            pltpu.VMEM((PAIRS // 2, LANES, LANES), BF16),
+            pltpu.VMEM((CELLS * PAIRS, LANES), F32),
+            pltpu.VMEM((TILES, PIECE, NC, LANES), F32),
+            pltpu.VMEM((CELLS, NEAR, LANES), F32),
+            pltpu.VMEM((CELLS, NEAR, LANES), F32),
+            pltpu.VMEM((TILES, PIECE, NC, LANES), F32),
+            pltpu.VMEM((2 * TILES * NC, PIECE * LANES), BF16),
+            pltpu.VMEM((TILES, PIECE, DC, LANES), F32),
+            pltpu.VMEM((2, LANES), F32),
+            pltpu.VMEM((TILES + 2, 2, LANES), F32),
+            pltpu.VMEM((1, LANES), F32),
+            pltpu.VMEM((BANDS, 1, LANES), F32),
+            dma((5,)),
+            dma((TILES + 2,)), dma((TILES + 2,)),
+            dma((TILES,)), dma((TILES,)),
+            dma((TILES,)), dma((TILES,)),
+            dma((2,)), dma((2,)),
+            dma((BANDS,)), dma((BANDS,)),
+        ],
+        compiler_params=pltpu.CompilerParams(
+            collective_id=0, has_side_effects=True, vmem_limit_bytes=40 * 2**20
+        ),
+        name="exchange",
+    )(
+        counts,
+        pair_patch,
+        pair_atm.reshape(1, PAIRS),
+        numerators.transpose(0, 2, 1),
+        patches.reshape(-1, LANES, LANES),
+    )
+
+
+def place_kernel(far_ref, near_ref, place_ref, out_ref):
+    put = place_ref[...].astype(BF16)
+    put2 = jnp.concatenate([put, put], axis=1)
+    rest = jnp.zeros((LANES - FAR0 - DC, PIECE * LANES), F32)
+
+    @pl.loop(0, TILES)
+    def _(m):
+        groups = [
+            jnp.concatenate([near_ref[i, m * PIECE + c] for c in range(PIECE)], axis=1)
+            for i in range(3)
+        ]
+        groups.append(jnp.concatenate([far_ref[m, c] for c in range(PIECE)], axis=1))
+        groups.append(rest)
+        high, low = split(jnp.concatenate(groups, axis=0))
+        total = jnp.dot(
+            put2, jnp.concatenate([high, low], axis=0), preferred_element_type=F32
+        )
+        for c in range(PIECE):
+            out_ref[pl.ds(m * PIECE + c, BLOCKS, stride=CELLS), :] = total[
+                :, c * LANES : (c + 1) * LANES
+            ]
+
+
+def place(far, near, put):
+    vmem = pl.BlockSpec(memory_space=pltpu.VMEM)
+    return pl.pallas_call(
+        place_kernel,
+        out_shape=jax.ShapeDtypeStruct((BLOCKS * CELLS, LANES), F32),
+        in_specs=[vmem, vmem, vmem],
+        out_specs=vmem,
+        compiler_params=pltpu.CompilerParams(vmem_limit_bytes=40 * 2**20),
+        name="place",
+    )(far, near, put)
 
 
 def shifted(value, axis, steps):
@@ -43,7 +505,7 @@
     return shifted((parcel[0], parcel[1]), "band", offset_by)
 
 
-def per_device(patches, pair_patch, pair_atm, numerators, counts):
+def long_route(patches, pair_patch, pair_atm, numerators, counts):
     pairs_here, patch_rows, cell_rows = numerators.shape
     flux_width = patches.shape[1]
     blocks_owned = CELLS_DEV // cell_rows
@@ -96,6 +558,15 @@
     return summed.reshape(blocks_owned * cell_rows, flux_width)
 
 
+def per_device(patches, pair_patch, pair_atm, numerators, counts):
+    far, near, put, flag = exchange(patches, pair_patch, pair_atm, numerators, counts)
+    return lax.cond(
+        flag[0] == 0,
+        lambda: place(far, near, put),
+        lambda: long_route(patches, pair_patch, pair_atm, numerators, counts),
+    )
+
+
 def solution(mesh):
     placed = (
         P(("band", "tile"), None),

time: 106 us -> 48.2 us (0.45)
  Pallas kernels: 0 us -> 46.3 us
  waiting for transfers between devices: 45.9 us -> 0 us
  starting transfers between devices: 24 us -> 0 us
  matrix products: 22.2 us -> 0 us
  local copies, waits for them, and re-layouts: 9.75 us -> 0.01 us
  other arithmetic: 2.95 us -> 0 us
    pallas_call x0 -> x2, Pallas kernels: none -> 46.3 us  [the longest x1 39.8 us: exchange(): pl.pallas_call(exchange_kernel, out_shape=(jax.ShapeDtypeStruct((TILES, P...]
    all_to_all x2 -> x0, waiting for transfers between devices: 45.4 us -> none  [the longest x1 45.4 us: per_device(): lax.all_to_all(payload.reshape(tile_count, bucket_size, -1), 'tile', spli...]
    dot_general x5 -> x0, matrix products: 22.2 us -> none  [the longest x3 10.9 us: pack(): jnp.dot(onehot.astype(jnp.float32), flattened, precision=lax.Precision.HI...]
    all_to_all x2 -> x0, starting transfers between devices: 15.2 us -> none  [the longest x1 7.99 us: per_device(): lax.all_to_all(labels.reshape(tile_count, bucket_size), 'tile', split_axi...]
    ppermute x4 -> x0, starting transfers between devices: 8.72 us -> none  [shifted(): lax.ppermute(value, axis, [(source, source + steps) for source in range(f...]
    reshape x3 -> x0, local copies, waits for them, and re-layouts: 5.53 us -> none  [the longest x1 2.75 us: per_device(): flattened = partial_value.reshape(pairs_here, cell_rows * flux_width)]
    gather x1 -> x0, local copies, waits for them, and re-layouts: 3.01 us -> none  [per_device(): chosen = grouped[pair_patch]]
    select_n x3 -> x0, other arithmetic: 1.35 us -> none  [the longest x1 0.67 us: per_device(): blocks_local = pair_atm % blocks_owned]
  transfers between devices with their start and end apart: 6 -> 0, of which waited for: 2 -> 0; matrix products, arithmetic and copies ran while one was open for 23% -> 0% of each run, Pallas kernels for 0% -> 0%
where the time goes in v1:
time: 48.2 us; the launch traced here: 48 us
  Pallas kernels  46.3 us (96%)
  between operations  1.4 us (3%)
    pallas_call x1, Pallas kernels, exchange(): pl.pallas_call(exchange_kernel, out_shape=(jax.ShapeDtypeStruct((TILES, P...  39.8 us
    pallas_call x1, Pallas kernels, place(): pl.pallas_call(place_kernel, out_shape=jax.ShapeDtypeStruct((BLOCKS * CEL...  6.56 us

profile of v1, /device:TPU:0, one launch (start us, length us, event | category | flops | bytes accessed | tf_op | source)
XLA Modules:
  0.0 48.0 jit_solution(12084741614247345016)
XLA Ops:
  0.7 0.0 copy-start
  0.7 0.0 copy-start.1
  0.7 0.0 copy-start.2
  0.7 39.8 %exchange.1 = (f32[16,2,72,128]{3,2,1,0:T(8,128)S(1)}, f32[3,32,16,128]{3,2,1,0:T(8,128)}, f32[128,128]{1,0:T(8,128)S(1)}, s32[1]{0:T(128)}) custom-call(s32[1]{0:T(128)S(6)} %copy.19.counts_ref, s32[128]{0:T(128)} %patch_ref.1, s32[1,128]{1,0:T(1,128)} %bitcast.20, s32[128,32,128]{2,1,0:T(8,128)} %bitcast.19, bf16[64,128,128]{2,1,0:T(8,128)(2,1)} %bitcast.17), custom_call_target="tpu_custom_call" | custom-call | tf_op jit(solution)/shard_map/exchange/pallas_call | solution.py:395
  41.2 0.0 copy-done
  41.2 0.0 copy-done.1
  41.2 0.0 copy-done.2
  41.2 6.8 %conditional.1 = (f32[4096,128]{1,0:T(8,128)}) conditional(s32[]{:T(128)} %bitcast.6, (s32[1]{0:T(128)}, s32[128]{0:T(128)S(1)}, s32[128,128,32]{1,2,0:T(8,128)}, bf16[8192,128]{1,0:T(8,128)(2,1)S(1)}, s32[128]{0:T(128)S(1)}) %tuple.29, (f32[16,2,72,128]{3,2,1,0:T(8,128)S(1)}, f32[3,32,16,128]{3,2,1,0:T(8,128)}, f32[128,128]{1,0:T(8,128)S(1)}) %tuple.12), branch_computations={%region_0.7_spmd, %region_7.8_spmd} | conditional | flops 3762688256 | bytes 57723524 | solution.py:563
  41.4 6.6 %place.1 = f32[4096,128]{1,0:T(8,128)} custom-call(f32[16,2,72,128]{3,2,1,0:T(8,128)S(1)} %get-tuple-element.29.far_ref, f32[3,32,16,128]{3,2,1,0:T(8,128)} %get-tuple-element.30.near_ref, f32[128,128]{1,0:T(8,128)S(1)} %get-tuple-element.31.place_ref), custom_call_target="tpu_custom_call" | custom-call | tf_op jit(solution)/shard_map/cond/branch_1_fun/place/pallas_call | solution.py:464
Async XLA Ops:
  0.7 40.5 %copy-start = (bf16[8192,128]{1,0:T(8,128)(2,1)S(1)}, bf16[8192,128]{1,0:T(8,128)(2,1)}, u32[]{:S(2)}) copy-start(bf16[8192,128]{1,0:T(8,128)(2,1)} %param.7) | copy-start | bytes 6291460
  0.7 40.5 %copy-start.1 = (s32[128]{0:T(128)S(1)}, s32[128]{0:T(128)}, u32[]{:S(2)}) copy-start(s32[128]{0:T(128)} %patch_ref.1) | copy-start | bytes 1540
  0.7 40.5 %copy-start.2 = (s32[128]{0:T(128)S(1)}, s32[128]{0:T(128)}, u32[]{:S(2)}) copy-start(s32[128]{0:T(128)} %param.9) | copy-start | bytes 1540

commit v2 on v1

--- a/solution.py
+++ b/solution.py
@@ -19,7 +19,8 @@
 NEAR = 16
 FAR0 = 3 * NEAR
 NC = 32
-DC = 72
+DC = 80
+NC_MID, DC_MID = 16, 72
 PIECE = CELLS // TILES
 MESH = pl.DeviceIdType.MESH
 F32, BF16, I32 = jnp.float32, jnp.bfloat16, jnp.int32
@@ -35,15 +36,16 @@
 
 
 def exchange_kernel(
-    counts_ref, patch_ref, atm_ref, num_hbm, patches_hbm,
-    far_ref, near_ref, place_ref, flag_ref,
-    num_v, pat_v, part, send_far, send_up, send_down, relay, stacked, parcel,
-    note, notes, alarm, alarms,
+    counts_ref, patch_hbm, atm_hbm, num_hbm, patches_hbm,
+    out_ref, flag_ref,
+    patch_ref, atm_ref, num_v, pat_v, part, send_far, send_up, send_down, relay, stacked,
+    parcel, far_ref, near_ref, note, notes, alarm, alarms,
     in_sem, note_send, note_recv, r_send, r_recv, q_send, q_recv,
     near_send, near_recv, alarm_send, alarm_recv,
 ):
     band, tile = lax.axis_index("band"), lax.axis_index("tile")
-    chunks = in_sem.shape[0] - 1
+    edge = (band == 0) | (band == BANDS - 1)
+    chunks = in_sem.shape[0] - 3
     rows = PAIRS // chunks
 
     def tile_at(k):
@@ -52,6 +54,19 @@
     def band_at(k):
         return lax.rem(band + k, BANDS)
 
+    def each_size(body):
+        @pl.when(edge)
+        def _():
+            body(NC, DC)
+
+        @pl.when(jnp.logical_not(edge))
+        def _():
+            body(NC_MID, DC_MID)
+
+    atm_copy = pltpu.make_async_copy(atm_hbm, atm_ref, in_sem.at[chunks + 1])
+    atm_copy.start()
+    patch_copy = pltpu.make_async_copy(patch_hbm, patch_ref, in_sem.at[chunks + 2])
+    patch_copy.start()
     pat_copy = pltpu.make_async_copy(patches_hbm, pat_v, in_sem.at[chunks])
     pat_copy.start()
     num_copies = [
@@ -79,6 +94,7 @@
     def column(row):
         return jnp.sum(jnp.where(lane == sub, row, 0.0), axis=1, keepdims=True)
 
+    atm_copy.wait()
     atm = atm_ref[...]
     live = lane1 < counts_ref[0]
     owner = atm >> 7
@@ -121,48 +137,12 @@
         notes[TILES + 1] = jnp.zeros((2, LANES), F32)
         near_ref[2] = jnp.zeros((CELLS, NEAR, LANES), F32)
 
-    pl.semaphore_wait(barrier, TILES + BANDS - 2)
-
-    def note_to(k):
-        return pltpu.make_async_remote_copy(
-            src_ref=note, dst_ref=notes.at[tile], send_sem=note_send.at[tile_at(k)],
-            recv_sem=note_recv.at[tile], device_id={"tile": tile_at(k)}, device_id_type=MESH,
-        )
-
-    def note_from(k):
-        source = tile_at(TILES - k)
-        return pltpu.make_async_remote_copy(
-            src_ref=note, dst_ref=notes.at[source], send_sem=note_send.at[source],
-            recv_sem=note_recv.at[source], device_id={"tile": source}, device_id_type=MESH,
-        )
-
-    def note_up():
-        return pltpu.make_async_remote_copy(
-            src_ref=note, dst_ref=notes.at[TILES], send_sem=note_send.at[TILES],
-            recv_sem=note_recv.at[TILES], device_id={"band": band_at(1)}, device_id_type=MESH,
-        )
-
-    def note_down():
-        return pltpu.make_async_remote_copy(
-            src_ref=note, dst_ref=notes.at[TILES + 1], send_sem=note_send.at[TILES + 1],
-            recv_sem=note_recv.at[TILES + 1], device_id={"band": band_at(BANDS - 1)},
-            device_id_type=MESH,
-        )
-
-    @pl.loop(1, TILES)
-    def _(k):
-        note_to(k).start()
-
-    @pl.when(band < BANDS - 1)
-    def _():
-        note_up().start()
-
-    @pl.when(band > 0)
-    def _():
-        note_down().start()
-
-    notes[tile] = note[...]
-
+    @pl.when(jnp.logical_not(edge))
+    def _():
+        relay[:, :, NC_MID:] = jnp.zeros((TILES, PIECE, NC - NC_MID, LANES), F32)
+        far_ref[:, :, DC_MID:] = jnp.zeros((TILES, PIECE, DC - DC_MID, LANES), F32)
+
+    patch_copy.wait()
     pat_copy.wait()
     for i in range(chunks):
         num_copies[i].wait()
@@ -175,6 +155,48 @@
                 weight, pat_v[patch_ref[g]], preferred_element_type=F32
             )
 
+    pl.semaphore_wait(barrier, TILES + BANDS - 2)
+
+    def note_to(k):
+        return pltpu.make_async_remote_copy(
+            src_ref=note, dst_ref=notes.at[tile], send_sem=note_send.at[tile_at(k)],
+            recv_sem=note_recv.at[tile], device_id={"tile": tile_at(k)}, device_id_type=MESH,
+        )
+
+    def note_from(k):
+        source = tile_at(TILES - k)
+        return pltpu.make_async_remote_copy(
+            src_ref=note, dst_ref=notes.at[source], send_sem=note_send.at[source],
+            recv_sem=note_recv.at[source], device_id={"tile": source}, device_id_type=MESH,
+        )
+
+    def note_up():
+        return pltpu.make_async_remote_copy(
+            src_ref=note, dst_ref=notes.at[TILES], send_sem=note_send.at[TILES],
+            recv_sem=note_recv.at[TILES], device_id={"band": band_at(1)}, device_id_type=MESH,
+        )
+
+    def note_down():
+        return pltpu.make_async_remote_copy(
+            src_ref=note, dst_ref=notes.at[TILES + 1], send_sem=note_send.at[TILES + 1],
+            recv_sem=note_recv.at[TILES + 1], device_id={"band": band_at(BANDS - 1)},
+            device_id_type=MESH,
+        )
+
+    @pl.loop(1, TILES)
+    def _(k):
+        note_to(k).start()
+
+    @pl.when(band < BANDS - 1)
+    def _():
+        note_up().start()
+
+    @pl.when(band > 0)
+    def _():
+        note_down().start()
+
+    notes[tile] = note[...]
+
     slot_sub = iota((FAR0 + NC, LANES), 0)
     pick = jnp.where(slot.astype(I32) == slot_sub, SCALE, 0.0).astype(BF16)
     pick2 = jnp.concatenate([pick, pick], axis=1)
@@ -192,23 +214,29 @@
             send_down[m * PIECE + c] = here[2 * NEAR : FAR0]
             send_far[m, c] = here[FAR0:]
 
-    def far_to(k):
-        return pltpu.make_async_remote_copy(
-            src_ref=send_far.at[tile_at(k)], dst_ref=relay.at[tile], send_sem=r_send.at[tile_at(k)],
-            recv_sem=r_recv.at[tile], device_id={"tile": tile_at(k)}, device_id_type=MESH,
-        )
-
-    def far_from(k):
+    def far_to(k, c, n):
+        return pltpu.make_async_remote_copy(
+            src_ref=send_far.at[tile_at(k), c, pl.ds(0, n)], dst_ref=relay.at[tile, c, pl.ds(0, n)],
+            send_sem=r_send.at[c, tile_at(k)], recv_sem=r_recv.at[c, tile],
+            device_id={"tile": tile_at(k)}, device_id_type=MESH,
+        )
+
+    def far_from(k, c, n):
         source = tile_at(TILES - k)
         return pltpu.make_async_remote_copy(
-            src_ref=send_far.at[source], dst_ref=relay.at[source], send_sem=r_send.at[source],
-            recv_sem=r_recv.at[source], device_id={"tile": source}, device_id_type=MESH,
+            src_ref=send_far.at[source, c, pl.ds(0, n)], dst_ref=relay.at[source, c, pl.ds(0, n)],
+            send_sem=r_send.at[c, source], recv_sem=r_recv.at[c, source],
+            device_id={"tile": source}, device_id_type=MESH,
         )
 
     @pl.loop(1, TILES)
     def _(k):
         slots_of(tile_at(k))
-        far_to(k).start()
+        each_size(lambda n, d: far_to(k, 0, n).start())
+
+    @pl.loop(1, TILES)
+    def _(k):
+        each_size(lambda n, d: far_to(k, 1, n).start())
 
     slots_of(tile)
     relay[tile] = send_far[tile]
@@ -267,10 +295,10 @@
     for s in range(1, TILES):
         most_far = jnp.maximum(most_far, notes[s, 1:2, :])
     over_far = jnp.max(
-        jnp.where(lane1 == LANES - 1, most_far - NC, 0.0), axis=1, keepdims=True
+        jnp.where(lane1 == LANES - 1, most_far - jnp.where(edge, NC, NC_MID).astype(F32), 0.0), axis=1, keepdims=True
     )
     load = jnp.sum(taken, axis=0, keepdims=True)
-    over_load = jnp.max(load - DC, axis=1, keepdims=True)
+    over_load = jnp.max(load - jnp.where(edge, DC, DC_MID).astype(F32), axis=1, keepdims=True)
     alarm[...] = jnp.broadcast_to(
         jnp.where((over_far > 0.0) | (over_load > 0.0), 1.0, 0.0), (1, LANES)
     )
@@ -312,47 +340,81 @@
     my_order = jnp.sum(jnp.where(mine, order, 0.0), axis=1, keepdims=True).astype(I32)
     is_near = (lane < FAR0) & (near_labels.astype(I32) == sub + 1)
     is_far = (lane >= FAR0) & (lane < FAR0 + DC) & (my_taken > 0.0) & (my_order == lane - FAR0)
-    place_ref[...] = jnp.where(is_near | is_far, 1.0, 0.0)
-
-    @pl.loop(1, TILES)
-    def _(k):
-        far_from(k).wait_recv()
-
-    for c in range(PIECE):
-        high, low = split(relay[:, c].reshape(entries, LANES))
-        stacked[:entries, c * LANES : (c + 1) * LANES] = high
-        stacked[entries:, c * LANES : (c + 1) * LANES] = low
+    put = jnp.where(is_near | is_far, 1.0, 0.0).astype(BF16)
+    put2 = jnp.concatenate([put, put], axis=1)
+
     depth_sub = iota((DC, entries), 0)
 
-    def blocks_of(owner_tile):
+    def blocks_of(owner_tile, c):
         hot = jnp.where(depth_sub + owner_tile * DC == goal, 1.0, 0.0).astype(BF16)
         return jnp.dot(
-            jnp.concatenate([hot, hot], axis=1), stacked[...], preferred_element_type=F32
-        )
-
-    def parcel_to(k):
-        return pltpu.make_async_remote_copy(
-            src_ref=parcel.at[tile_at(k)], dst_ref=far_ref.at[tile], send_sem=q_send.at[tile_at(k)],
-            recv_sem=q_recv.at[tile], device_id={"tile": tile_at(k)}, device_id_type=MESH,
-        )
-
-    def parcel_from(k):
+            jnp.concatenate([hot, hot], axis=1), stacked[c], preferred_element_type=F32
+        )
+
+    def parcel_to(k, c, d):
+        return pltpu.make_async_remote_copy(
+            src_ref=parcel.at[tile_at(k), c, pl.ds(0, d)], dst_ref=far_ref.at[tile, c, pl.ds(0, d)],
+            send_sem=q_send.at[c, tile_at(k)], recv_sem=q_recv.at[c, tile],
+            device_id={"tile": tile_at(k)}, device_id_type=MESH,
+        )
+
+    def parcel_from(k, c, d):
         source = tile_at(TILES - k)
         return pltpu.make_async_remote_copy(
-            src_ref=parcel.at[source], dst_ref=far_ref.at[source], send_sem=q_send.at[source],
-            recv_sem=q_recv.at[source], device_id={"tile": source}, device_id_type=MESH,
-        )
+            src_ref=parcel.at[source, c, pl.ds(0, d)], dst_ref=far_ref.at[source, c, pl.ds(0, d)],
+            send_sem=q_send.at[c, source], recv_sem=q_recv.at[c, source],
+            device_id={"tile": source}, device_id_type=MESH,
+        )
+
+    for c in range(PIECE):
+
+        @pl.loop(1, TILES)
+        def _(k):
+            each_size(lambda n, d: far_from(k, c, n).wait_recv())
+
+        high, low = split(relay[:, c].reshape(entries, LANES))
+        stacked[c, :entries] = high
+        stacked[c, entries:] = low
+
+        @pl.loop(1, TILES)
+        def _(k):
+            parcel[tile_at(k), c] = blocks_of(tile_at(k), c)
+            each_size(lambda n, d: parcel_to(k, c, d).start())
+
+    for c in range(PIECE):
+        far_ref[tile, c] = blocks_of(tile, c)
+
+    @pl.when(band > 0)
+    def _():
+        near_up().wait_recv()
+
+    @pl.when(band < BANDS - 1)
+    def _():
+        near_down().wait_recv()
+
+    def cells_of(m):
+        groups = [
+            jnp.concatenate([near_ref[i, m * PIECE + c] for c in range(PIECE)], axis=1)
+            for i in range(3)
+        ]
+        groups.append(jnp.concatenate([far_ref[m, c] for c in range(PIECE)], axis=1))
+        total = jnp.dot(
+            put2,
+            jnp.concatenate(split(jnp.concatenate(groups, axis=0)), axis=0),
+            preferred_element_type=F32,
+        )
+        for c in range(PIECE):
+            out_ref[pl.ds(m * PIECE + c, BLOCKS, stride=CELLS), :] = total[
+                :, c * LANES : (c + 1) * LANES
+            ]
+
+    cells_of(tile)
 
     @pl.loop(1, TILES)
     def _(k):
-        total = blocks_of(tile_at(k))
         for c in range(PIECE):
-            parcel[tile_at(k), c] = total[:, c * LANES : (c + 1) * LANES]
-        parcel_to(k).start()
-
-    own = blocks_of(tile)
-    for c in range(PIECE):
-        far_ref[tile, c] = own[:, c * LANES : (c + 1) * LANES]
+            each_size(lambda n, d: parcel_from(k, c, d).wait_recv())
+        cells_of(tile_at(TILES - k))
 
     @pl.loop(1, BANDS)
     def _(k):
@@ -362,13 +424,11 @@
 
     @pl.when(band > 0)
     def _():
-        near_up().wait_recv()
         note_down().wait_send()
         near_down().wait_send()
 
     @pl.when(band < BANDS - 1)
     def _():
-        near_down().wait_recv()
         note_up().wait_send()
         near_up().wait_send()
 
@@ -379,12 +439,9 @@
     @pl.loop(1, TILES)
     def _(k):
         note_to(k).wait_send()
-        far_to(k).wait_send()
-        parcel_from(k).wait_recv()
-
-    @pl.loop(1, TILES)
-    def _(k):
-        parcel_to(k).wait_send()
+        for c in range(PIECE):
+            each_size(lambda n, d: far_to(k, c, n).wait_send())
+            each_size(lambda n, d: parcel_to(k, c, d).wait_send())
 
 
 def exchange(patches, pair_patch, pair_atm, numerators, counts):
@@ -395,14 +452,14 @@
     return pl.pallas_call(
         exchange_kernel,
         out_shape=(
-            jax.ShapeDtypeStruct((TILES, PIECE, DC, LANES), F32),
-            jax.ShapeDtypeStruct((3, CELLS, NEAR, LANES), F32),
-            jax.ShapeDtypeStruct((BLOCKS, LANES), F32),
+            jax.ShapeDtypeStruct((BLOCKS * CELLS, LANES), F32),
             jax.ShapeDtypeStruct((1,), I32),
         ),
-        in_specs=[smem, smem, vmem, anywhere, anywhere],
-        out_specs=(vmem, vmem, vmem, smem),
+        in_specs=[smem, anywhere, anywhere, anywhere, anywhere],
+        out_specs=(vmem, smem),
         scratch_shapes=[
+            pltpu.SMEM((PAIRS,), I32),
+            pltpu.VMEM((1, PAIRS), I32),
             pltpu.VMEM((PAIRS, CELLS, LANES), I32),
             pltpu.VMEM((PAIRS // 2, LANES, LANES), BF16),
             pltpu.VMEM((CELLS * PAIRS, LANES), F32),
@@ -410,16 +467,18 @@
             pltpu.VMEM((CELLS, NEAR, LANES), F32),
             pltpu.VMEM((CELLS, NEAR, LANES), F32),
             pltpu.VMEM((TILES, PIECE, NC, LANES), F32),
-            pltpu.VMEM((2 * TILES * NC, PIECE * LANES), BF16),
+            pltpu.VMEM((PIECE, 2 * TILES * NC, LANES), BF16),
             pltpu.VMEM((TILES, PIECE, DC, LANES), F32),
+            pltpu.VMEM((TILES, PIECE, DC, LANES), F32),
+            pltpu.VMEM((3, CELLS, NEAR, LANES), F32),
             pltpu.VMEM((2, LANES), F32),
             pltpu.VMEM((TILES + 2, 2, LANES), F32),
             pltpu.VMEM((1, LANES), F32),
             pltpu.VMEM((BANDS, 1, LANES), F32),
-            dma((5,)),
+            dma((7,)),
             dma((TILES + 2,)), dma((TILES + 2,)),
-            dma((TILES,)), dma((TILES,)),
-            dma((TILES,)), dma((TILES,)),
+            dma((PIECE, TILES)), dma((PIECE, TILES)),
+            dma((PIECE, TILES)), dma((PIECE, TILES)),
             dma((2,)), dma((2,)),
             dma((BANDS,)), dma((BANDS,)),
         ],
@@ -436,39 +495,31 @@
     )
 
 
-def place_kernel(far_ref, near_ref, place_ref, out_ref):
-    put = place_ref[...].astype(BF16)
-    put2 = jnp.concatenate([put, put], axis=1)
-    rest = jnp.zeros((LANES - FAR0 - DC, PIECE * LANES), F32)
-
-    @pl.loop(0, TILES)
-    def _(m):
-        groups = [
-            jnp.concatenate([near_ref[i, m * PIECE + c] for c in range(PIECE)], axis=1)
-            for i in range(3)
-        ]
-        groups.append(jnp.concatenate([far_ref[m, c] for c in range(PIECE)], axis=1))
-        groups.append(rest)
-        high, low = split(jnp.concatenate(groups, axis=0))
-        total = jnp.dot(
-            put2, jnp.concatenate([high, low], axis=0), preferred_element_type=F32
-        )
-        for c in range(PIECE):
-            out_ref[pl.ds(m * PIECE + c, BLOCKS, stride=CELLS), :] = total[
-                :, c * LANES : (c + 1) * LANES
-            ]
-
-
-def place(far, near, put):
-    vmem = pl.BlockSpec(memory_space=pltpu.VMEM)
+def put_kernel(total_ref, out_ref, sem):
+    parts = sem.shape[0]
+    rows = total_ref.shape[0] // parts
+    copies = [
+        pltpu.make_async_copy(
+            total_ref.at[pl.ds(i * rows, rows)], out_ref.at[pl.ds(i * rows, rows)], sem.at[i]
+        )
+        for i in range(parts)
+    ]
+    for copy in copies:
+        copy.start()
+    for copy in copies:
+        copy.wait()
+
+
+def put(total):
     return pl.pallas_call(
-        place_kernel,
-        out_shape=jax.ShapeDtypeStruct((BLOCKS * CELLS, LANES), F32),
-        in_specs=[vmem, vmem, vmem],
-        out_specs=vmem,
-        compiler_params=pltpu.CompilerParams(vmem_limit_bytes=40 * 2**20),
-        name="place",
-    )(far, near, put)
+        put_kernel,
+        out_shape=jax.ShapeDtypeStruct(total.shape, F32),
+        in_specs=[pl.BlockSpec(memory_space=pltpu.VMEM)],
+        out_specs=pl.BlockSpec(memory_space=pl.ANY),
+        scratch_shapes=[pltpu.SemaphoreType.DMA((4,))],
+        compiler_params=pltpu.CompilerParams(vmem_limit_bytes=8 * 2**20),
+        name="put",
+    )(total)
 
 
 def shifted(value, axis, steps):
@@ -559,10 +610,10 @@
 
 
 def per_device(patches, pair_patch, pair_atm, numerators, counts):
-    far, near, put, flag = exchange(patches, pair_patch, pair_atm, numerators, counts)
+    total, flag = exchange(patches, pair_patch, pair_atm, numerators, counts)
     return lax.cond(
         flag[0] == 0,
-        lambda: place(far, near, put),
+        lambda: put(total),
         lambda: long_route(patches, pair_patch, pair_atm, numerators, counts),
     )
 

time: 48.2 us -> 42.9 us (0.89)
  Pallas kernels: 46.3 us -> 40.5 us
    pallas_call x2, Pallas kernels: 46.3 us -> 40.5 us  [the longest x1 37.6 us: exchange(): pl.pallas_call(exchange_kernel, out_shape=(jax.ShapeDtypeStruct((BLOCKS *...]
where the time goes in v2:
time: 42.9 us; the launch traced here: 42.4 us
  Pallas kernels  40.5 us (94%)
  between operations  1.58 us (4%)
    pallas_call x1, Pallas kernels, exchange(): pl.pallas_call(exchange_kernel, out_shape=(jax.ShapeDtypeStruct((BLOCKS *...  37.6 us
    pallas_call x1, Pallas kernels, put(): pl.pallas_call(put_kernel, out_shape=jax.ShapeDtypeStruct(total.shape, F3...  2.94 us

profile of v2, /device:TPU:0, one launch (start us, length us, event | category | flops | bytes accessed | tf_op | source)
XLA Modules:
  0.0 42.4 jit_solution(1489417032388672773)
XLA Ops:
  0.7 0.0 copy-start
  0.7 0.0 copy-start.1
  0.7 0.0 copy-start.2
  0.7 37.6 %exchange.1 = (f32[4096,128]{1,0:T(8,128)}, s32[1]{0:T(128)}) custom-call(s32[1]{0:T(128)S(6)} %copy.19.counts_ref, s32[128]{0:T(128)} %patch_hbm.1, s32[1,128]{1,0:T(1,128)} %bitcast.20, s32[128,32,128]{2,1,0:T(8,128)} %bitcast.19, bf16[64,128,128]{2,1,0:T(8,128)(2,1)} %bitcast.17), custom_call_target="tpu_custom_call" | custom-call | tf_op jit(solution)/shard_map/exchange/pallas_call | solution.py:452
  39.0 0.0 copy-done
  39.0 0.0 copy-done.1
  39.0 0.0 copy-done.2
  39.0 3.2 %conditional.1 = (f32[4096,128]{1,0:T(8,128)}) conditional(s32[]{:T(128)} %bitcast.6, (s32[1]{0:T(128)}, s32[128]{0:T(128)S(1)}, s32[128,128,32]{1,2,0:T(8,128)}, bf16[8192,128]{1,0:T(8,128)(2,1)S(1)}, s32[128]{0:T(128)S(1)}) %tuple.28, f32[4096,128]{1,0:T(8,128)} %get-tuple-element.27), branch_computations={%region_0.7_spmd, %region_7.8_spmd} | conditional | flops 3762688256 | bytes 57723524 | solution.py:614
  39.2 2.9 %put.1 = f32[4096,128]{1,0:T(8,128)} custom-call(f32[4096,128]{1,0:T(8,128)} %total_ref), custom_call_target="tpu_custom_call" | custom-call | tf_op jit(solution)/shard_map/cond/branch_1_fun/put/pallas_call | solution.py:514
Async XLA Ops:
  0.7 38.3 %copy-start = (bf16[8192,128]{1,0:T(8,128)(2,1)S(1)}, bf16[8192,128]{1,0:T(8,128)(2,1)}, u32[]{:S(2)}) copy-start(bf16[8192,128]{1,0:T(8,128)(2,1)} %param.7) | copy-start | bytes 6291460
  0.7 38.3 %copy-start.1 = (s32[128]{0:T(128)S(1)}, s32[128]{0:T(128)}, u32[]{:S(2)}) copy-start(s32[128]{0:T(128)} %patch_hbm.1) | copy-start | bytes 1540
  0.7 38.3 %copy-start.2 = (s32[128]{0:T(128)S(1)}, s32[128]{0:T(128)}, u32[]{:S(2)}) copy-start(s32[128]{0:T(128)} %param.9) | copy-start | bytes 1540

commit v3 on v2

--- a/solution.py
+++ b/solution.py
@@ -18,6 +18,9 @@
 BLOCKS = 128
 NEAR = 16
 FAR0 = 3 * NEAR
+SLOTS = 128 + 8
+NONE = 128
+GROUP = 4
 NC = 32
 DC = 80
 NC_MID, DC_MID = 16, 72
@@ -37,10 +40,10 @@
 
 def exchange_kernel(
     counts_ref, patch_hbm, atm_hbm, num_hbm, patches_hbm,
-    out_ref, flag_ref,
-    patch_ref, atm_ref, num_v, pat_v, part, send_far, send_up, send_down, relay, stacked,
-    parcel, far_ref, near_ref, note, notes, alarm, alarms,
-    in_sem, note_send, note_recv, r_send, r_recv, q_send, q_recv,
+    all_ref, index_ref, flag_ref,
+    patch_ref, atm_ref, num_v, pat_v, table, table_s, part, send_far, send_up, send_down,
+    relay, stacked, parcel, note, notes, alarm, alarms,
+    in_sem, table_sem, note_send, note_recv, r_send, r_recv, q_send, q_recv,
     near_send, near_recv, alarm_send, alarm_recv,
 ):
     band, tile = lax.axis_index("band"), lax.axis_index("tile")
@@ -115,6 +118,20 @@
     slot = jnp.where(live, base + rank, -1.0)
     slot_c = column(slot).astype(I32)
     leads = first_c > 0.0
+    later = jnp.sum(jnp.where(same & (sub > lane), 1.0, 0.0), axis=0, keepdims=True)
+    last_c = column(jnp.where(live & (later == 0.0), 1.0, 0.0))
+    turn = jnp.where(live, slot, 2.0 * PAIRS)
+    turn_c = column(turn)
+    before = (turn_c < turn) | ((turn_c == turn) & (sub < lane))
+    place_c = column(jnp.sum(jnp.where(before, 1.0, 0.0), axis=0, keepdims=True)).astype(I32)
+    at = place_c == lane
+    table[0:1, :] = jnp.sum(jnp.where(at, sub, 0), axis=0, keepdims=True)
+    joins_c = column(earlier).astype(I32)
+    table[1:2, :] = jnp.sum(jnp.where(at & (joins_c > 0), 1, 0), axis=0, keepdims=True)
+    ends = (last_c > 0.0) & (slot_c == lane)
+    table[2:3, :] = PAIRS + jnp.sum(jnp.where(ends, place_c - PAIRS, 0), axis=0, keepdims=True)
+    table_copy = pltpu.make_async_copy(table, table_s, table_sem)
+    table_copy.start()
     key_i = key_c.astype(I32)
     far_lane = slot_c - FAR0 + NC * lax.rem(tile, 4)
     in_far = leads & (slot_c >= FAR0) & (slot_c < FAR0 + NC)
@@ -130,30 +147,41 @@
     @pl.when(band == 0)
     def _():
         notes[TILES] = jnp.zeros((2, LANES), F32)
-        near_ref[1] = jnp.zeros((CELLS, NEAR, LANES), F32)
 
     @pl.when(band == BANDS - 1)
     def _():
         notes[TILES + 1] = jnp.zeros((2, LANES), F32)
-        near_ref[2] = jnp.zeros((CELLS, NEAR, LANES), F32)
 
     @pl.when(jnp.logical_not(edge))
     def _():
         relay[:, :, NC_MID:] = jnp.zeros((TILES, PIECE, NC - NC_MID, LANES), F32)
-        far_ref[:, :, DC_MID:] = jnp.zeros((TILES, PIECE, DC - DC_MID, LANES), F32)
+
+    all_ref[:, NONE:] = jnp.zeros((CELLS, SLOTS - NONE, LANES), F32)
+    part[PAIRS] = jnp.zeros((CELLS, LANES), F32)
 
     patch_copy.wait()
+    table_copy.wait()
     pat_copy.wait()
-    for i in range(chunks):
-        num_copies[i].wait()
-
-        @pl.loop(0, rows, unroll=8)
-        def _(j):
-            g = i * rows + j
-            weight = num_v[g].astype(F32).astype(BF16)
-            part[pl.ds(g, CELLS, stride=PAIRS), :] = jnp.dot(
-                weight, pat_v[patch_ref[g]], preferred_element_type=F32
-            )
+    for copy in num_copies:
+        copy.wait()
+
+    def add_pair(i, total):
+        g = table_s[0, i]
+        weight = (num_v[g].astype(F32) * SCALE).astype(BF16)
+        product = jnp.dot(weight, pat_v[patch_ref[g]], preferred_element_type=F32)
+        total = jnp.where(table_s[1, i] > 0, total, 0.0) + product
+        part[i] = total
+        return total
+
+    lax.fori_loop(0, PAIRS, add_pair, jnp.zeros((CELLS, LANES), F32), unroll=8)
+
+    self_rows = all_ref.reshape(CELLS * SLOTS, LANES)
+    up_rows = send_up.reshape(CELLS * NEAR, LANES)
+    down_rows = send_down.reshape(CELLS * NEAR, LANES)
+
+    @pl.loop(0, NC, unroll=4)
+    def _(j):
+        send_far[pl.ds(j, CELLS, stride=NC), :] = part[table_s[2, FAR0 + j]]
 
     pl.semaphore_wait(barrier, TILES + BANDS - 2)
 
@@ -197,26 +225,9 @@
 
     notes[tile] = note[...]
 
-    slot_sub = iota((FAR0 + NC, LANES), 0)
-    pick = jnp.where(slot.astype(I32) == slot_sub, SCALE, 0.0).astype(BF16)
-    pick2 = jnp.concatenate([pick, pick], axis=1)
-
-    def slots_of(m):
-        both = part[pl.ds(m * PIECE * PAIRS, PIECE * PAIRS), :]
-        wide = jnp.concatenate([both[:PAIRS], both[PAIRS:]], axis=1)
-        total = jnp.dot(
-            pick2, jnp.concatenate(split(wide), axis=0), preferred_element_type=F32
-        )
-        for c in range(PIECE):
-            here = total[:, c * LANES : (c + 1) * LANES]
-            near_ref[0, m * PIECE + c] = here[:NEAR]
-            send_up[m * PIECE + c] = here[NEAR : 2 * NEAR]
-            send_down[m * PIECE + c] = here[2 * NEAR : FAR0]
-            send_far[m, c] = here[FAR0:]
-
     def far_to(k, c, n):
         return pltpu.make_async_remote_copy(
-            src_ref=send_far.at[tile_at(k), c, pl.ds(0, n)], dst_ref=relay.at[tile, c, pl.ds(0, n)],
+            src_ref=send_far.at[pl.ds((tile_at(k) * PIECE + c) * NC, n)], dst_ref=relay.at[tile, c, pl.ds(0, n)],
             send_sem=r_send.at[c, tile_at(k)], recv_sem=r_recv.at[c, tile],
             device_id={"tile": tile_at(k)}, device_id_type=MESH,
         )
@@ -224,32 +235,34 @@
     def far_from(k, c, n):
         source = tile_at(TILES - k)
         return pltpu.make_async_remote_copy(
-            src_ref=send_far.at[source, c, pl.ds(0, n)], dst_ref=relay.at[source, c, pl.ds(0, n)],
+            src_ref=send_far.at[pl.ds((source * PIECE + c) * NC, n)], dst_ref=relay.at[source, c, pl.ds(0, n)],
             send_sem=r_send.at[c, source], recv_sem=r_recv.at[c, source],
             device_id={"tile": source}, device_id_type=MESH,
         )
 
-    @pl.loop(1, TILES)
-    def _(k):
-        slots_of(tile_at(k))
-        each_size(lambda n, d: far_to(k, 0, n).start())
-
-    @pl.loop(1, TILES)
-    def _(k):
-        each_size(lambda n, d: far_to(k, 1, n).start())
-
-    slots_of(tile)
-    relay[tile] = send_far[tile]
+    for c in range(PIECE):
+
+        @pl.loop(1, TILES)
+        def _(k):
+            each_size(lambda n, d: far_to(k, c, n).start())
+
+    for c in range(PIECE):
+        relay[tile, c] = send_far[pl.ds((tile * PIECE + c) * NC, NC), :]
+
+    @pl.loop(0, NEAR, unroll=4)
+    def _(j):
+        up_rows[pl.ds(j, CELLS, stride=NEAR), :] = part[table_s[2, NEAR + j]]
+        down_rows[pl.ds(j, CELLS, stride=NEAR), :] = part[table_s[2, 2 * NEAR + j]]
 
     def near_up():
         return pltpu.make_async_remote_copy(
-            src_ref=send_up, dst_ref=near_ref.at[1], send_sem=near_send.at[0],
+            src_ref=send_up, dst_ref=all_ref.at[:, pl.ds(NEAR, NEAR)], send_sem=near_send.at[0],
             recv_sem=near_recv.at[0], device_id={"band": band_at(1)}, device_id_type=MESH,
         )
 
     def near_down():
         return pltpu.make_async_remote_copy(
-            src_ref=send_down, dst_ref=near_ref.at[2], send_sem=near_send.at[1],
+            src_ref=send_down, dst_ref=all_ref.at[:, pl.ds(2 * NEAR, NEAR)], send_sem=near_send.at[1],
             recv_sem=near_recv.at[1], device_id={"band": band_at(BANDS - 1)}, device_id_type=MESH,
         )
 
@@ -260,6 +273,10 @@
     @pl.when(band > 0)
     def _():
         near_down().start()
+
+    @pl.loop(0, NEAR, unroll=4)
+    def _(j):
+        self_rows[pl.ds(j, CELLS, stride=SLOTS), :] = part[table_s[2, j]]
 
     @pl.loop(1, TILES)
     def _(k):
@@ -335,33 +352,40 @@
         note[1:2, :],
         jnp.where(lane1 < 2 * NEAR, notes[TILES, 1:2, :], notes[TILES + 1, 1:2, :]),
     )
+    here = column(near_labels).astype(I32) == lane + 1
+    for i in range(3):
+        found = here & (sub >= i * NEAR) & (sub < (i + 1) * NEAR)
+        index_ref[i : i + 1, :] = NONE + jnp.sum(
+            jnp.where(found, sub - NONE, 0), axis=0, keepdims=True
+        )
     mine = iota((BLOCKS, TILES), 1) == tile
-    my_taken = jnp.sum(jnp.where(mine, taken, 0.0), axis=1, keepdims=True)
-    my_order = jnp.sum(jnp.where(mine, order, 0.0), axis=1, keepdims=True).astype(I32)
-    is_near = (lane < FAR0) & (near_labels.astype(I32) == sub + 1)
-    is_far = (lane >= FAR0) & (lane < FAR0 + DC) & (my_taken > 0.0) & (my_order == lane - FAR0)
-    put = jnp.where(is_near | is_far, 1.0, 0.0).astype(BF16)
-    put2 = jnp.concatenate([put, put], axis=1)
-
-    depth_sub = iota((DC, entries), 0)
-
-    def blocks_of(owner_tile, c):
-        hot = jnp.where(depth_sub + owner_tile * DC == goal, 1.0, 0.0).astype(BF16)
+    my_row = jnp.sum(
+        jnp.where(mine & (taken > 0.0), order + FAR0 - NONE, 0.0), axis=1, keepdims=True
+    )
+    index_ref[3:4, :] = NONE + jnp.sum(
+        jnp.where(lane == sub, my_row, 0.0), axis=0, keepdims=True
+    ).astype(I32)
+
+    depth_sub = iota((GROUP * DC, entries), 0)
+
+    def blocks_of(group, c):
+        hot = jnp.where(depth_sub + group * (GROUP * DC) == goal, 1.0, 0.0).astype(BF16)
         return jnp.dot(
             jnp.concatenate([hot, hot], axis=1), stacked[c], preferred_element_type=F32
-        )
-
-    def parcel_to(k, c, d):
-        return pltpu.make_async_remote_copy(
-            src_ref=parcel.at[tile_at(k), c, pl.ds(0, d)], dst_ref=far_ref.at[tile, c, pl.ds(0, d)],
-            send_sem=q_send.at[c, tile_at(k)], recv_sem=q_recv.at[c, tile],
-            device_id={"tile": tile_at(k)}, device_id_type=MESH,
-        )
-
-    def parcel_from(k, c, d):
-        source = tile_at(TILES - k)
-        return pltpu.make_async_remote_copy(
-            src_ref=parcel.at[source, c, pl.ds(0, d)], dst_ref=far_ref.at[source, c, pl.ds(0, d)],
+        ).reshape(GROUP, DC, LANES)
+
+    def parcel_to(target, c, d):
+        return pltpu.make_async_remote_copy(
+            src_ref=parcel.at[target, c, pl.ds(0, d)],
+            dst_ref=all_ref.at[tile * PIECE + c, pl.ds(FAR0, d)],
+            send_sem=q_send.at[c, target], recv_sem=q_recv.at[c, tile],
+            device_id={"tile": target}, device_id_type=MESH,
+        )
+
+    def parcel_from(source, c, d):
+        return pltpu.make_async_remote_copy(
+            src_ref=parcel.at[source, c, pl.ds(0, d)],
+            dst_ref=all_ref.at[source * PIECE + c, pl.ds(FAR0, d)],
             send_sem=q_send.at[c, source], recv_sem=q_recv.at[c, source],
             device_id={"tile": source}, device_id_type=MESH,
         )
@@ -376,59 +400,37 @@
         stacked[c, :entries] = high
         stacked[c, entries:] = low
 
-        @pl.loop(1, TILES)
-        def _(k):
-            parcel[tile_at(k), c] = blocks_of(tile_at(k), c)
-            each_size(lambda n, d: parcel_to(k, c, d).start())
+        @pl.loop(1, GROUP + 1)
+        def _(q):
+            group = lax.rem(tile // GROUP + q, GROUP)
+            parcel[pl.ds(group * GROUP, GROUP), c] = blocks_of(group, c)
+
+            @pl.loop(0, GROUP)
+            def _(k):
+                target = group * GROUP + lax.rem(tile + k, GROUP)
+
+                @pl.when(target != tile)
+                def _():
+                    each_size(lambda n, d: parcel_to(target, c, d).start())
 
     for c in range(PIECE):
-        far_ref[tile, c] = blocks_of(tile, c)
+        all_ref[tile * PIECE + c, FAR0:NONE] = parcel[tile, c]
+
+    @pl.loop(1, BANDS)
+    def _(k):
+        alarm_from(k).wait_recv()
+
+    flag_ref[0] = jnp.max(alarms[...]).astype(I32)
 
     @pl.when(band > 0)
     def _():
         near_up().wait_recv()
-
-    @pl.when(band < BANDS - 1)
-    def _():
-        near_down().wait_recv()
-
-    def cells_of(m):
-        groups = [
-            jnp.concatenate([near_ref[i, m * PIECE + c] for c in range(PIECE)], axis=1)
-            for i in range(3)
-        ]
-        groups.append(jnp.concatenate([far_ref[m, c] for c in range(PIECE)], axis=1))
-        total = jnp.dot(
-            put2,
-            jnp.concatenate(split(jnp.concatenate(groups, axis=0)), axis=0),
-            preferred_element_type=F32,
-        )
-        for c in range(PIECE):
-            out_ref[pl.ds(m * PIECE + c, BLOCKS, stride=CELLS), :] = total[
-                :, c * LANES : (c + 1) * LANES
-            ]
-
-    cells_of(tile)
-
-    @pl.loop(1, TILES)
-    def _(k):
-        for c in range(PIECE):
-            each_size(lambda n, d: parcel_from(k, c, d).wait_recv())
-        cells_of(tile_at(TILES - k))
-
-    @pl.loop(1, BANDS)
-    def _(k):
-        alarm_from(k).wait_recv()
-
-    flag_ref[0] = jnp.max(alarms[...]).astype(I32)
-
-    @pl.when(band > 0)
-    def _():
         note_down().wait_send()
         near_down().wait_send()
 
     @pl.when(band < BANDS - 1)
     def _():
+        near_down().wait_recv()
         note_up().wait_send()
         near_up().wait_send()
 
@@ -441,7 +443,8 @@
         note_to(k).wait_send()
         for c in range(PIECE):
             each_size(lambda n, d: far_to(k, c, n).wait_send())
-            each_size(lambda n, d: parcel_to(k, c, d).wait_send())
+            each_size(lambda n, d: parcel_to(tile_at(k), c, d).wait_send())
+            each_size(lambda n, d: parcel_from(tile_at(k), c, d).wait_recv())
 
 
 def exchange(patches, pair_patch, pair_atm, numerators, counts):
@@ -452,30 +455,31 @@
     return pl.pallas_call(
         exchange_kernel,
         out_shape=(
-            jax.ShapeDtypeStruct((BLOCKS * CELLS, LANES), F32),
+            jax.ShapeDtypeStruct((CELLS, SLOTS, LANES), F32),
+            jax.ShapeDtypeStruct((4, BLOCKS), I32),
             jax.ShapeDtypeStruct((1,), I32),
         ),
         in_specs=[smem, anywhere, anywhere, anywhere, anywhere],
-        out_specs=(vmem, smem),
+        out_specs=(vmem, vmem, smem),
         scratch_shapes=[
             pltpu.SMEM((PAIRS,), I32),
             pltpu.VMEM((1, PAIRS), I32),
             pltpu.VMEM((PAIRS, CELLS, LANES), I32),
             pltpu.VMEM((PAIRS // 2, LANES, LANES), BF16),
-            pltpu.VMEM((CELLS * PAIRS, LANES), F32),
-            pltpu.VMEM((TILES, PIECE, NC, LANES), F32),
+            pltpu.VMEM((8, PAIRS), I32),
+            pltpu.SMEM((8, PAIRS), I32),
+            pltpu.VMEM((PAIRS + 1, CELLS, LANES), F32),
+            pltpu.VMEM((CELLS * NC, LANES), F32),
             pltpu.VMEM((CELLS, NEAR, LANES), F32),
             pltpu.VMEM((CELLS, NEAR, LANES), F32),
             pltpu.VMEM((TILES, PIECE, NC, LANES), F32),
             pltpu.VMEM((PIECE, 2 * TILES * NC, LANES), BF16),
             pltpu.VMEM((TILES, PIECE, DC, LANES), F32),
-            pltpu.VMEM((TILES, PIECE, DC, LANES), F32),
-            pltpu.VMEM((3, CELLS, NEAR, LANES), F32),
             pltpu.VMEM((2, LANES), F32),
             pltpu.VMEM((TILES + 2, 2, LANES), F32),
             pltpu.VMEM((1, LANES), F32),
             pltpu.VMEM((BANDS, 1, LANES), F32),
-            dma((7,)),
+            dma((7,)), dma,
             dma((TILES + 2,)), dma((TILES + 2,)),
             dma((PIECE, TILES)), dma((PIECE, TILES)),
             dma((PIECE, TILES)), dma((PIECE, TILES)),
@@ -483,7 +487,7 @@
             dma((BANDS,)), dma((BANDS,)),
         ],
         compiler_params=pltpu.CompilerParams(
-            collective_id=0, has_side_effects=True, vmem_limit_bytes=40 * 2**20
+            collective_id=0, has_side_effects=True, vmem_limit_bytes=24 * 2**20
         ),
         name="exchange",
     )(
@@ -495,31 +499,42 @@
     )
 
 
-def put_kernel(total_ref, out_ref, sem):
+def place_kernel(index_ref, all_ref, out_ref, total, sem):
     parts = sem.shape[0]
-    rows = total_ref.shape[0] // parts
-    copies = [
-        pltpu.make_async_copy(
-            total_ref.at[pl.ds(i * rows, rows)], out_ref.at[pl.ds(i * rows, rows)], sem.at[i]
-        )
-        for i in range(parts)
-    ]
-    for copy in copies:
-        copy.start()
+    blocks = BLOCKS // parts
+    copies = []
+    for i in range(parts):
+
+        @pl.loop(i * blocks, (i + 1) * blocks, unroll=4)
+        def _(a):
+            rows = [
+                all_ref[pl.ds(index_ref[r, a], CELLS, stride=SLOTS), :] for r in range(4)
+            ]
+            total[pl.ds(a * CELLS, CELLS), :] = (rows[0] + rows[1]) + (rows[2] + rows[3])
+
+        here = pl.ds(i * blocks * CELLS, blocks * CELLS)
+        copies.append(pltpu.make_async_copy(total.at[here], out_ref.at[here], sem.at[i]))
+        copies[-1].start()
     for copy in copies:
         copy.wait()
 
 
-def put(total):
+def place(everything, index):
     return pl.pallas_call(
-        put_kernel,
-        out_shape=jax.ShapeDtypeStruct(total.shape, F32),
-        in_specs=[pl.BlockSpec(memory_space=pltpu.VMEM)],
+        place_kernel,
+        out_shape=jax.ShapeDtypeStruct((BLOCKS * CELLS, LANES), F32),
+        in_specs=[
+            pl.BlockSpec(memory_space=pltpu.SMEM),
+            pl.BlockSpec(memory_space=pltpu.VMEM),
+        ],
         out_specs=pl.BlockSpec(memory_space=pl.ANY),
-        scratch_shapes=[pltpu.SemaphoreType.DMA((4,))],
-        compiler_params=pltpu.CompilerParams(vmem_limit_bytes=8 * 2**20),
-        name="put",
-    )(total)
+        scratch_shapes=[
+            pltpu.VMEM((BLOCKS * CELLS, LANES), F32),
+            pltpu.SemaphoreType.DMA((8,)),
+        ],
+        compiler_params=pltpu.CompilerParams(vmem_limit_bytes=16 * 2**20),
+        name="place",
+    )(index, everything.reshape(CELLS * SLOTS, LANES))
 
 
 def shifted(value, axis, steps):
@@ -610,10 +625,10 @@
 
 
 def per_device(patches, pair_patch, pair_atm, numerators, counts):
-    total, flag = exchange(patches, pair_patch, pair_atm, numerators, counts)
+    everything, index, flag = exchange(patches, pair_patch, pair_atm, numerators, counts)
     return lax.cond(
         flag[0] == 0,
-        lambda: put(total),
+        lambda: place(everything, index),
         lambda: long_route(patches, pair_patch, pair_atm, numerators, counts),
     )
 

time: 42.9 us -> 41 us (0.956)
  Pallas kernels: 40.5 us -> 38.4 us
    pallas_call x2, Pallas kernels: 40.5 us -> 38.4 us  [the longest x1 33.6 us: exchange(): pl.pallas_call(exchange_kernel, out_shape=(jax.ShapeDtypeStruct((CELLS, S...]
where the time goes in v3:
time: 41 us; the launch traced here: 40.3 us
  Pallas kernels  38.4 us (94%)
  between operations  1.58 us (4%)
    pallas_call x1, Pallas kernels, exchange(): pl.pallas_call(exchange_kernel, out_shape=(jax.ShapeDtypeStruct((CELLS, S...  33.6 us
    pallas_call x1, Pallas kernels, place(): pl.pallas_call(place_kernel, out_shape=jax.ShapeDtypeStruct((BLOCKS * CEL...  4.84 us

profile of v3, /device:TPU:0, one launch (start us, length us, event | category | flops | bytes accessed | tf_op | source)
XLA Modules:
  0.0 40.3 jit_solution(392863865988148477)
XLA Ops:
  0.7 0.0 copy-start
  0.7 0.0 copy-start.1
  0.7 0.0 copy-start.2
  0.7 33.6 %exchange.1 = (f32[32,136,128]{2,1,0:T(8,128)}, s32[4,128]{1,0:T(4,128)S(1)}, s32[1]{0:T(128)}) custom-call(s32[1]{0:T(128)S(6)} %copy.19.counts_ref, s32[128]{0:T(128)} %patch_hbm.1, s32[1,128]{1,0:T(1,128)} %bitcast.22, s32[128,32,128]{2,1,0:T(8,128)} %bitcast.20, bf16[64,128,128]{2,1,0:T(8,128)(2,1)} %bitcast.18), custom_call_target="tpu_custom_call" | custom-call | tf_op jit(solution)/shard_map/exchange/pallas_call | solution.py:455
  35.0 0.0 copy-done
  35.0 0.0 copy-done.1
  35.0 0.0 copy-done.2
  35.0 5.1 %conditional.1 = (f32[4096,128]{1,0:T(8,128)}) conditional(s32[]{:T(128)} %bitcast.7, (s32[1]{0:T(128)}, s32[128]{0:T(128)S(1)}, s32[128,128,32]{1,2,0:T(8,128)}, bf16[8192,128]{1,0:T(8,128)(2,1)S(1)}, s32[128]{0:T(128)S(1)}) %tuple.29, (f32[32,136,128]{2,1,0:T(8,128)}, s32[4,128]{1,0:T(4,128)S(1)}) %tuple.12), branch_computations={%region_0.7_spmd, %region_7.8_spmd} | conditional | flops 3762688256 | bytes 57723524 | solution.py:629
  35.2 4.8 %place.1 = f32[4096,128]{1,0:T(8,128)} custom-call(s32[4,128]{1,0:T(4,128)S(1)} %get-tuple-element.27.index_ref, f32[4352,128]{1,0:T(8,128)} %bitcast.21), custom_call_target="tpu_custom_call" | custom-call | tf_op jit(solution)/shard_map/cond/branch_1_fun/place/pallas_call | solution.py:523
Async XLA Ops:
  0.7 34.3 %copy-start = (bf16[8192,128]{1,0:T(8,128)(2,1)S(1)}, bf16[8192,128]{1,0:T(8,128)(2,1)}, u32[]{:S(2)}) copy-start(bf16[8192,128]{1,0:T(8,128)(2,1)} %param.7) | copy-start | bytes 6291460
  0.7 34.3 %copy-start.1 = (s32[128]{0:T(128)S(1)}, s32[128]{0:T(128)}, u32[]{:S(2)}) copy-start(s32[128]{0:T(128)} %patch_hbm.1) | copy-start | bytes 1540
  0.7 34.3 %copy-start.2 = (s32[128]{0:T(128)S(1)}, s32[128]{0:T(128)}, u32[]{:S(2)}) copy-start(s32[128]{0:T(128)} %param.9) | copy-start | bytes 1540

commit v4 on v3

--- a/solution.py
+++ b/solution.py
@@ -18,12 +18,11 @@
 BLOCKS = 128
 NEAR = 16
 FAR0 = 3 * NEAR
-SLOTS = 128 + 8
-NONE = 128
 GROUP = 4
 NC = 32
 DC = 80
 NC_MID, DC_MID = 16, 72
+NEAR_STEP, NC_STEP, DC_STEP = NEAR + 4, NC + 4, DC + 4
 PIECE = CELLS // TILES
 MESH = pl.DeviceIdType.MESH
 F32, BF16, I32 = jnp.float32, jnp.bfloat16, jnp.int32
@@ -40,8 +39,8 @@
 
 def exchange_kernel(
     counts_ref, patch_hbm, atm_hbm, num_hbm, patches_hbm,
-    all_ref, index_ref, flag_ref,
-    patch_ref, atm_ref, num_v, pat_v, table, table_s, part, send_far, send_up, send_down,
+    far_ref, near_ref, index_s, flag_ref,
+    index_ref, patch_ref, atm_ref, num_v, pat_v, table, table_s, part, send_far, send_up, send_down,
     relay, stacked, parcel, note, notes, alarm, alarms,
     in_sem, table_sem, note_send, note_recv, r_send, r_recv, q_send, q_recv,
     near_send, near_recv, alarm_send, alarm_recv,
@@ -147,16 +146,24 @@
     @pl.when(band == 0)
     def _():
         notes[TILES] = jnp.zeros((2, LANES), F32)
+        near_ref[1] = jnp.zeros((CELLS * NEAR_STEP, LANES), F32)
 
     @pl.when(band == BANDS - 1)
     def _():
         notes[TILES + 1] = jnp.zeros((2, LANES), F32)
+        near_ref[2] = jnp.zeros((CELLS * NEAR_STEP, LANES), F32)
 
     @pl.when(jnp.logical_not(edge))
     def _():
         relay[:, :, NC_MID:] = jnp.zeros((TILES, PIECE, NC - NC_MID, LANES), F32)
 
-    all_ref[:, NONE:] = jnp.zeros((CELLS, SLOTS - NONE, LANES), F32)
+    @pl.loop(0, CELLS, unroll=4)
+    def _(cell):
+        far_ref[pl.ds(cell * DC_STEP + DC, 4), :] = jnp.zeros((4, LANES), F32)
+        near_ref[0, pl.ds(cell * NEAR_STEP + NEAR, 4), :] = jnp.zeros((4, LANES), F32)
+        send_up[pl.ds(cell * NEAR_STEP + NEAR, 4), :] = jnp.zeros((4, LANES), F32)
+        send_down[pl.ds(cell * NEAR_STEP + NEAR, 4), :] = jnp.zeros((4, LANES), F32)
+
     part[PAIRS] = jnp.zeros((CELLS, LANES), F32)
 
     patch_copy.wait()
@@ -175,13 +182,9 @@
 
     lax.fori_loop(0, PAIRS, add_pair, jnp.zeros((CELLS, LANES), F32), unroll=8)
 
-    self_rows = all_ref.reshape(CELLS * SLOTS, LANES)
-    up_rows = send_up.reshape(CELLS * NEAR, LANES)
-    down_rows = send_down.reshape(CELLS * NEAR, LANES)
-
     @pl.loop(0, NC, unroll=4)
     def _(j):
-        send_far[pl.ds(j, CELLS, stride=NC), :] = part[table_s[2, FAR0 + j]]
+        send_far[pl.ds(j, CELLS, stride=NC_STEP), :] = part[table_s[2, FAR0 + j]]
 
     pl.semaphore_wait(barrier, TILES + BANDS - 2)
 
@@ -227,7 +230,7 @@
 
     def far_to(k, c, n):
         return pltpu.make_async_remote_copy(
-            src_ref=send_far.at[pl.ds((tile_at(k) * PIECE + c) * NC, n)], dst_ref=relay.at[tile, c, pl.ds(0, n)],
+            src_ref=send_far.at[pl.ds((tile_at(k) * PIECE + c) * NC_STEP, n)], dst_ref=relay.at[tile, c, pl.ds(0, n)],
             send_sem=r_send.at[c, tile_at(k)], recv_sem=r_recv.at[c, tile],
             device_id={"tile": tile_at(k)}, device_id_type=MESH,
         )
@@ -235,7 +238,7 @@
     def far_from(k, c, n):
         source = tile_at(TILES - k)
         return pltpu.make_async_remote_copy(
-            src_ref=send_far.at[pl.ds((source * PIECE + c) * NC, n)], dst_ref=relay.at[source, c, pl.ds(0, n)],
+            src_ref=send_far.at[pl.ds((source * PIECE + c) * NC_STEP, n)], dst_ref=relay.at[source, c, pl.ds(0, n)],
             send_sem=r_send.at[c, source], recv_sem=r_recv.at[c, source],
             device_id={"tile": source}, device_id_type=MESH,
         )
@@ -247,22 +250,22 @@
             each_size(lambda n, d: far_to(k, c, n).start())
 
     for c in range(PIECE):
-        relay[tile, c] = send_far[pl.ds((tile * PIECE + c) * NC, NC), :]
+        relay[tile, c] = send_far[pl.ds((tile * PIECE + c) * NC_STEP, NC), :]
 
     @pl.loop(0, NEAR, unroll=4)
     def _(j):
-        up_rows[pl.ds(j, CELLS, stride=NEAR), :] = part[table_s[2, NEAR + j]]
-        down_rows[pl.ds(j, CELLS, stride=NEAR), :] = part[table_s[2, 2 * NEAR + j]]
+        send_up[pl.ds(j, CELLS, stride=NEAR_STEP), :] = part[table_s[2, NEAR + j]]
+        send_down[pl.ds(j, CELLS, stride=NEAR_STEP), :] = part[table_s[2, 2 * NEAR + j]]
 
     def near_up():
         return pltpu.make_async_remote_copy(
-            src_ref=send_up, dst_ref=all_ref.at[:, pl.ds(NEAR, NEAR)], send_sem=near_send.at[0],
+            src_ref=send_up, dst_ref=near_ref.at[1], send_sem=near_send.at[0],
             recv_sem=near_recv.at[0], device_id={"band": band_at(1)}, device_id_type=MESH,
         )
 
     def near_down():
         return pltpu.make_async_remote_copy(
-            src_ref=send_down, dst_ref=all_ref.at[:, pl.ds(2 * NEAR, NEAR)], send_sem=near_send.at[1],
+            src_ref=send_down, dst_ref=near_ref.at[2], send_sem=near_send.at[1],
             recv_sem=near_recv.at[1], device_id={"band": band_at(BANDS - 1)}, device_id_type=MESH,
         )
 
@@ -276,7 +279,7 @@
 
     @pl.loop(0, NEAR, unroll=4)
     def _(j):
-        self_rows[pl.ds(j, CELLS, stride=SLOTS), :] = part[table_s[2, j]]
+        near_ref[0, pl.ds(j, CELLS, stride=NEAR_STEP), :] = part[table_s[2, j]]
 
     @pl.loop(1, TILES)
     def _(k):
@@ -355,16 +358,19 @@
     here = column(near_labels).astype(I32) == lane + 1
     for i in range(3):
         found = here & (sub >= i * NEAR) & (sub < (i + 1) * NEAR)
-        index_ref[i : i + 1, :] = NONE + jnp.sum(
-            jnp.where(found, sub - NONE, 0), axis=0, keepdims=True
+        index_ref[i : i + 1, :] = NEAR + jnp.sum(
+            jnp.where(found, sub - (i + 1) * NEAR, 0), axis=0, keepdims=True
         )
     mine = iota((BLOCKS, TILES), 1) == tile
     my_row = jnp.sum(
-        jnp.where(mine & (taken > 0.0), order + FAR0 - NONE, 0.0), axis=1, keepdims=True
-    )
-    index_ref[3:4, :] = NONE + jnp.sum(
+        jnp.where(mine & (taken > 0.0), order - DC, 0.0), axis=1, keepdims=True
+    )
+    index_ref[3:4, :] = DC + jnp.sum(
         jnp.where(lane == sub, my_row, 0.0), axis=0, keepdims=True
     ).astype(I32)
+
+    index_copy = pltpu.make_async_copy(index_ref, index_s, table_sem)
+    index_copy.start()
 
     depth_sub = iota((GROUP * DC, entries), 0)
 
@@ -377,7 +383,7 @@
     def parcel_to(target, c, d):
         return pltpu.make_async_remote_copy(
             src_ref=parcel.at[target, c, pl.ds(0, d)],
-            dst_ref=all_ref.at[tile * PIECE + c, pl.ds(FAR0, d)],
+            dst_ref=far_ref.at[pl.ds((tile * PIECE + c) * DC_STEP, d)],
             send_sem=q_send.at[c, target], recv_sem=q_recv.at[c, tile],
             device_id={"tile": target}, device_id_type=MESH,
         )
@@ -385,7 +391,7 @@
     def parcel_from(source, c, d):
         return pltpu.make_async_remote_copy(
             src_ref=parcel.at[source, c, pl.ds(0, d)],
-            dst_ref=all_ref.at[source * PIECE + c, pl.ds(FAR0, d)],
+            dst_ref=far_ref.at[pl.ds((source * PIECE + c) * DC_STEP, d)],
             send_sem=q_send.at[c, source], recv_sem=q_recv.at[c, source],
             device_id={"tile": source}, device_id_type=MESH,
         )
@@ -414,12 +420,13 @@
                     each_size(lambda n, d: parcel_to(target, c, d).start())
 
     for c in range(PIECE):
-        all_ref[tile * PIECE + c, FAR0:NONE] = parcel[tile, c]
+        far_ref[pl.ds((tile * PIECE + c) * DC_STEP, DC), :] = parcel[tile, c]
 
     @pl.loop(1, BANDS)
     def _(k):
         alarm_from(k).wait_recv()
 
+    index_copy.wait()
     flag_ref[0] = jnp.max(alarms[...]).astype(I32)
 
     @pl.when(band > 0)
@@ -455,13 +462,15 @@
     return pl.pallas_call(
         exchange_kernel,
         out_shape=(
-            jax.ShapeDtypeStruct((CELLS, SLOTS, LANES), F32),
-            jax.ShapeDtypeStruct((4, BLOCKS), I32),
-            jax.ShapeDtypeStruct((1,), I32),
+            pltpu.VMEM((CELLS * DC_STEP, LANES), F32),
+            pltpu.VMEM((3, CELLS * NEAR_STEP, LANES), F32),
+            pltpu.SMEM((4, BLOCKS), I32),
+            pltpu.SMEM((1,), I32),
         ),
         in_specs=[smem, anywhere, anywhere, anywhere, anywhere],
-        out_specs=(vmem, vmem, smem),
+        out_specs=(vmem, vmem, smem, smem),
         scratch_shapes=[
+            pltpu.VMEM((4, BLOCKS), I32),
             pltpu.SMEM((PAIRS,), I32),
             pltpu.VMEM((1, PAIRS), I32),
             pltpu.VMEM((PAIRS, CELLS, LANES), I32),
@@ -469,9 +478,9 @@
             pltpu.VMEM((8, PAIRS), I32),
             pltpu.SMEM((8, PAIRS), I32),
             pltpu.VMEM((PAIRS + 1, CELLS, LANES), F32),
-            pltpu.VMEM((CELLS * NC, LANES), F32),
-            pltpu.VMEM((CELLS, NEAR, LANES), F32),
-            pltpu.VMEM((CELLS, NEAR, LANES), F32),
+            pltpu.VMEM((CELLS * NC_STEP, LANES), F32),
+            pltpu.VMEM((CELLS * NEAR_STEP, LANES), F32),
+            pltpu.VMEM((CELLS * NEAR_STEP, LANES), F32),
             pltpu.VMEM((TILES, PIECE, NC, LANES), F32),
             pltpu.VMEM((PIECE, 2 * TILES * NC, LANES), BF16),
             pltpu.VMEM((TILES, PIECE, DC, LANES), F32),
@@ -499,7 +508,7 @@
     )
 
 
-def place_kernel(index_ref, all_ref, out_ref, total, sem):
+def place_kernel(index_ref, far_ref, near_ref, out_ref, total, sem):
     parts = sem.shape[0]
     blocks = BLOCKS // parts
     copies = []
@@ -507,10 +516,12 @@
 
         @pl.loop(i * blocks, (i + 1) * blocks, unroll=4)
         def _(a):
-            rows = [
-                all_ref[pl.ds(index_ref[r, a], CELLS, stride=SLOTS), :] for r in range(4)
+            near = [
+                near_ref[r, pl.ds(index_ref[r, a], CELLS, stride=NEAR_STEP), :]
+                for r in range(3)
             ]
-            total[pl.ds(a * CELLS, CELLS), :] = (rows[0] + rows[1]) + (rows[2] + rows[3])
+            far = far_ref[pl.ds(index_ref[3, a], CELLS, stride=DC_STEP), :]
+            total[pl.ds(a * CELLS, CELLS), :] = (near[0] + near[1]) + (near[2] + far)
 
         here = pl.ds(i * blocks * CELLS, blocks * CELLS)
         copies.append(pltpu.make_async_copy(total.at[here], out_ref.at[here], sem.at[i]))
@@ -519,14 +530,12 @@
         copy.wait()
 
 
-def place(everything, index):
+def place(far, near, index):
+    vmem = pl.BlockSpec(memory_space=pltpu.VMEM)
     return pl.pallas_call(
         place_kernel,
         out_shape=jax.ShapeDtypeStruct((BLOCKS * CELLS, LANES), F32),
-        in_specs=[
-            pl.BlockSpec(memory_space=pltpu.SMEM),
-            pl.BlockSpec(memory_space=pltpu.VMEM),
-        ],
+        in_specs=[pl.BlockSpec(memory_space=pltpu.SMEM), vmem, vmem],
         out_specs=pl.BlockSpec(memory_space=pl.ANY),
         scratch_shapes=[
             pltpu.VMEM((BLOCKS * CELLS, LANES), F32),
@@ -534,7 +543,7 @@
         ],
         compiler_params=pltpu.CompilerParams(vmem_limit_bytes=16 * 2**20),
         name="place",
-    )(index, everything.reshape(CELLS * SLOTS, LANES))
+    )(index, far, near)
 
 
 def shifted(value, axis, steps):
@@ -625,10 +634,10 @@
 
 
 def per_device(patches, pair_patch, pair_atm, numerators, counts):
-    everything, index, flag = exchange(patches, pair_patch, pair_atm, numerators, counts)
+    far, near, index, flag = exchange(patches, pair_patch, pair_atm, numerators, counts)
     return lax.cond(
         flag[0] == 0,
-        lambda: place(everything, index),
+        lambda: place(far, near, index),
         lambda: long_route(patches, pair_patch, pair_atm, numerators, counts),
     )
 

time: 41 us -> 35.5 us (0.87)
  Pallas kernels: 38.4 us -> 33.7 us
  between operations: 1.58 us -> 0.88 us
    pallas_call x1, Pallas kernels: 4.84 us -> 2.08 us  [place(): pl.pallas_call(place_kernel, out_shape=jax.ShapeDtypeStruct((BLOCKS * CEL...]
    pallas_call x1, Pallas kernels: 33.6 us -> 31.7 us  [exchange(): pl.pallas_call(exchange_kernel, out_shape=(pltpu.VMEM((CELLS * DC_STEP, L...]
where the time goes in v4:
time: 35.5 us; the launch traced here: 34.9 us
  Pallas kernels  33.7 us (95%)
  between operations  0.88 us (2%)
    pallas_call x1, Pallas kernels, exchange(): pl.pallas_call(exchange_kernel, out_shape=(pltpu.VMEM((CELLS * DC_STEP, L...  31.7 us
    pallas_call x1, Pallas kernels, place(): pl.pallas_call(place_kernel, out_shape=jax.ShapeDtypeStruct((BLOCKS * CEL...  2.08 us

profile of v4, /device:TPU:0, one launch (start us, length us, event | category | flops | bytes accessed | tf_op | source)
XLA Modules:
  0.0 34.9 jit_solution(5587761998554967030)
XLA Ops:
  0.7 0.0 copy-start
  0.7 0.0 copy-start.1
  0.7 31.7 %exchange.1 = (f32[2688,128]{1,0:T(8,128)S(1)}, f32[3,640,128]{2,1,0:T(8,128)S(1)}, s32[4,128]{1,0:T(4,128)S(4)}, s32[1]{0:T(128)S(4)}) custom-call(s32[1]{0:T(128)S(6)} %copy.19.counts_ref, s32[128]{0:T(128)} %patch_hbm.1, s32[1,128]{1,0:T(1,128)} %bitcast.20, s32[128,32,128]{2,1,0:T(8,128)} %bitcast.19, bf16[64,128,128]{2,1,0:T(8,128)(2,1)} %bitcast.17), custom_call_target="tpu_custom_call" | custom-call | tf_op jit(solution)/shard_map/exchange/pallas_call | solution.py:462
  32.4 0.0 copy-done
  32.4 0.0 copy-done.1
  32.4 2.3 %conditional.1 = (f32[4096,128]{1,0:T(8,128)}) conditional(s32[]{:T(128)} %bitcast.6, (s32[1]{0:T(128)}, s32[128]{0:T(128)S(1)}, s32[128,128,32]{1,2,0:T(8,128)}, bf16[8192,128]{1,0:T(8,128)(2,1)}, s32[128]{0:T(128)S(1)}) %tuple.28, (s32[4,128]{1,0:T(4,128)S(4)}, f32[2688,128]{1,0:T(8,128)S(1)}, f32[3,640,128]{2,1,0:T(8,128)S(1)}) %tuple.12), branch_computations={%region_0.7_spmd, %region_7.8_spmd} | conditional | flops 3762688256 | bytes 57723524 | solution.py:638
  32.6 2.1 %place.1 = f32[4096,128]{1,0:T(8,128)} custom-call(s32[4,128]{1,0:T(4,128)S(4)} %get-tuple-element.29.index_ref, f32[2688,128]{1,0:T(8,128)S(1)} %get-tuple-element.30.far_ref, f32[3,640,128]{2,1,0:T(8,128)S(1)} %get-tuple-element.31.near_ref), custom_call_target="tpu_custom_call" | custom-call | tf_op jit(solution)/shard_map/cond/branch_1_fun/place/pallas_call | solution.py:535
Async XLA Ops:
  0.7 31.7 %copy-start = (s32[128]{0:T(128)S(1)}, s32[128]{0:T(128)}, u32[]{:S(2)}) copy-start(s32[128]{0:T(128)} %patch_hbm.1) | copy-start | bytes 1540
  0.7 31.7 %copy-start.1 = (s32[128]{0:T(128)S(1)}, s32[128]{0:T(128)}, u32[]{:S(2)}) copy-start(s32[128]{0:T(128)} %param.9) | copy-start | bytes 1540
